TPU v7x, 32 devices: a whole 2x2x4 slice. The times are simulated.
32 devices in a mesh: rows: 8 (over z, x), probe: 4 (over y, core).
Axes of the slice: x: 2, y: 2, z: 4, core: 2. Of those that a mesh axis runs over, the one named last changes fastest.
Arguments:
- start_block: float32 [8, 32768], P('probe', 'rows'), may hold values from -6 to 6
- blocks: bfloat16 [1024, 128, 128], P('rows'), may hold values from 0 to 3, as said below
- block_rows: int32 [1024], P('rows'), may hold values from 0 to 31
- block_cols: int32 [1024], P('rows'), may hold values from 0 to 63
- counts: int32 [8], P('rows'), may hold values from 32 to 128, as said below
- boundary: int32 [2, 16384], P(None, 'rows'), may hold values from 0 to 4095, as said below
Outputs:
- basis: float32 [8, 32768], P('probe', 'rows')
- alpha_blocks: float32 [3, 8, 8], replicated
- beta_blocks: float32 [3, 8, 8], replicated
Inputs may be any that keep to these rules, and one draw needn't show every extreme that they name: `blocks`: nonnegative edge weights, most entries zero. `counts`: one or more partitions have all 128 slots live. `boundary`: the 2048 entries of one list for one partition are distinct rows of that partition.
All inputs are finite; a program needn't handle non-finite values.
Results may differ from a plain program's by a relative error of at most 0.00525.
Values may be sent and summed in bfloat16 or wider, within the bound.
A program may use at most 64 MiB of HBM per device.

v0:
```python
import functools

import jax
import jax.numpy as jnp
from jax import lax
from jax.experimental import pallas as pl
from jax.experimental.pallas import tpu as pltpu
from jax.sharding import PartitionSpec as P

STEPS = 3
LANES = 128
UNROLL = 16
MESH = pl.DeviceIdType.MESH


def kernel(
    n_rows, n_probe, node_total,
    start_ref, tiles_hbm, perm_r, keep_r, end_r, perm_c, keep_c, end_c, rows_ref, cols_ref, bound_ref, inverse_ref,
    basis_ref, alpha_ref, beta_ref,
    tiles, gathered, current, previous, image, inv_root, scaled, own, extended, halo_send, ret_send, ret_recv,
    row_sums, col_sums, gram_send, gram_recv,
    tile_sem, start_send, start_recv, halo_ssem, halo_rsem, ret_ssem, ret_rsem, gram_ssem, gram_rsem,
):
    me = lax.axis_index("rows")
    my_probe = lax.axis_index("probe")
    slots = tiles.shape[0]
    nb = current.shape[0] // 8
    nh = nb // 2
    probes_dev = start_ref.shape[0]
    lower = lax.rem(me + n_rows - 1, n_rows)
    upper = lax.rem(me + 1, n_rows)

    tile_copy = pltpu.make_async_copy(tiles_hbm, tiles, tile_sem)
    tile_copy.start()

    barrier = pltpu.get_barrier_semaphore()
    for off in range(1, n_probe):
        peer = lax.rem(my_probe + off, n_probe)
        pl.semaphore_signal(barrier, inc=1, device_id={"probe": peer}, device_id_type=MESH)

    def greet(off, carry):
        peer = lax.rem(me + off, n_rows)
        pl.semaphore_signal(barrier, inc=1, device_id={"rows": peer}, device_id_type=MESH)
        return carry

    lax.fori_loop(1, n_rows, greet, 0)
    pl.semaphore_wait(barrier, n_probe - 1 + n_rows - 1)

    def start_copy(off):
        peer = lax.rem(my_probe + off, n_probe)
        return pltpu.make_async_remote_copy(
            src_ref=start_ref,
            dst_ref=gathered.at[pl.ds(my_probe * probes_dev, probes_dev)],
            send_sem=start_send.at[off],
            recv_sem=start_recv.at[off],
            device_id={"probe": peer},
            device_id_type=MESH,
        )

    for off in range(1, n_probe):
        start_copy(off).start()
    gathered[pl.ds(my_probe * probes_dev, probes_dev)] = start_ref[...]

    def row_of(ref, block, probe):
        return jnp.broadcast_to(ref[pl.ds(block * 8 + probe, 1), :], (8, LANES))

    def block_of(ref, block):
        return ref[pl.ds(pl.multiple_of(block * 8, 8), 8), :]

    def put_block(ref, block, value):
        ref[pl.ds(pl.multiple_of(block * 8, 8), 8), :] = value

    lane = lax.broadcasted_iota(jnp.int32, (8, LANES), 1)
    sub = lax.broadcasted_iota(jnp.int32, (8, LANES), 0)
    zero = jnp.zeros((8, LANES), jnp.float32)

    def fold(accs):
        gram = zero
        for q in range(8):
            gram = jnp.where(lane == q, jnp.sum(accs[q], axis=1, keepdims=True), gram)
        return gram

    def gram_copy(index, off):
        peer = lax.rem(me + off, n_rows)
        return pltpu.make_async_remote_copy(
            src_ref=gram_send.at[index],
            dst_ref=gram_recv.at[index, me],
            send_sem=gram_ssem.at[index, off],
            recv_sem=gram_rsem.at[index, off],
            device_id={"rows": peer},
            device_id_type=MESH,
        )

    def gram_begin(index, gram):
        gram_send[index] = gram
        gram_recv[index, me] = gram

        def send(off, carry):
            gram_copy(index, off).start()
            return carry

        lax.fori_loop(1, n_rows, send, 0)

    def gram_end(index):
        def wait(off, carry):
            gram_copy(index, off).wait()
            return carry

        lax.fori_loop(1, n_rows, wait, 0)
        return jnp.sum(gram_recv[index], axis=0) * (1.0 / node_total)

    def factorise(gram):
        work = jnp.where(lane < 8, gram, jnp.where(lane == sub + 8, 1.0, 0.0))
        factor = zero
        scale = zero
        for j in range(8):
            column = jnp.broadcast_to(work[:, j : j + 1], (8, LANES))
            row = jnp.broadcast_to(work[j : j + 1, :], (8, LANES))
            pivot = jnp.broadcast_to(row[:, j : j + 1], (8, LANES))
            root = jnp.sqrt(pivot)
            factor = jnp.where((lane == j) & (sub >= j), column / root, factor)
            scale = jnp.where(sub == j, 1.0 / root, scale)
            work = work - jnp.where(sub > j, column / pivot, 0.0) * row
        work = work * scale
        return factor, work

    def columns_of(matrix, first):
        return [jnp.broadcast_to(matrix[:, first + q : first + q + 1], (8, LANES)) for q in range(8)]

    def col_products(lhs_of):
        def body(turn, acc):
            ys = []
            for u in range(UNROLL):
                m = turn * UNROLL + u
                t = perm_c[m]
                ys.append(jnp.dot(lhs_of(rows_ref, t), tiles[t], preferred_element_type=jnp.float32))
            for u in range(UNROLL):
                m = turn * UNROLL + u
                acc = acc * keep_c[m] + ys[u]
                col_sums[m] = acc
            return acc

        lax.fori_loop(0, slots // UNROLL, body, zero)

    def row_products(lhs_of):
        def body(turn, acc):
            ys = []
            for u in range(UNROLL):
                m = turn * UNROLL + u
                t = perm_r[m]
                ys.append(
                    lax.dot_general(
                        lhs_of(cols_ref, t), tiles[t], (((1,), (1,)), ((), ())), preferred_element_type=jnp.float32
                    )
                )
            for u in range(UNROLL):
                m = turn * UNROLL + u
                acc = acc * keep_r[m] + ys[u]
                row_sums[m] = acc
            return acc

        lax.fori_loop(0, slots // UNROLL, body, zero)

    def ret_copies(index):
        return [
            pltpu.make_async_remote_copy(
                src_ref=ret_send.at[index, side],
                dst_ref=ret_recv.at[index, 1 - side],
                send_sem=ret_ssem.at[index, side],
                recv_sem=ret_rsem.at[index, side],
                device_id={"rows": lower if side == 0 else upper},
                device_id_type=MESH,
            )
            for side in range(2)
        ]

    def halo_copies(index):
        return [
            pltpu.make_async_remote_copy(
                src_ref=halo_send.at[index, side],
                dst_ref=extended.at[index, pl.ds(nb + (1 - side) * nh, nh)],
                send_sem=halo_ssem.at[index, side],
                recv_sem=halo_rsem.at[index, side],
                device_id={"rows": lower if side == 0 else upper},
                device_id_type=MESH,
            )
            for side in range(2)
        ]

    def send_returns(index):
        def body(c, carry):
            for side in range(2):
                ret_send[index, side, c] = col_sums[end_c[nb + side * nh + c]]
            return carry

        lax.fori_loop(0, nh, body, 0)
        for copy in ret_copies(index):
            copy.start()

    def summed(index, block):
        total = row_sums[end_r[block]] + col_sums[end_c[block]]
        for side in range(2):
            where = jnp.broadcast_to(inverse_ref[pl.ds(side * nb + block, 1), :], (8, LANES))
            spot = jnp.bitwise_and(where, LANES - 1)
            source = jnp.right_shift(where, 7)
            found = zero
            for s in range(nh):
                picked = jnp.take_along_axis(ret_recv[index, side, s], spot, axis=1, mode="promise_in_bounds")
                found = jnp.where(source == s, picked, found)
            total = total + found
        return total

    row_sums[slots] = zero
    col_sums[slots] = zero

    for off in range(1, n_probe):
        start_copy(off).wait()

    def take_start(block, accs):
        value = jnp.stack([gathered[p, pl.ds(block, 1), :] for p in range(8)], axis=0).reshape(8, LANES)
        put_block(image, block, value)
        return accs

    lax.fori_loop(0, nb, take_start, 0)

    def gram_of(left, right):
        def body(block, accs):
            value = block_of(left, block)
            return tuple(accs[q] + value * row_of(right, block, q) for q in range(8))

        return fold(lax.fori_loop(0, nb, body, (zero,) * 8, unroll=2))

    gram_begin(0, gram_of(image, image))

    tile_copy.wait()
    ones = jnp.ones((8, LANES), jnp.bfloat16)
    col_products(lambda ref, t: ones)
    send_returns(0)
    row_products(lambda ref, t: ones)
    for copy in ret_copies(0):
        copy.wait()

    def degree_block(block, carry):
        put_block(inv_root, block, 1.0 / jnp.sqrt(1.0 + summed(0, block)))
        return carry

    lax.fori_loop(0, nb, degree_block, 0)

    factor, work = factorise(gram_end(0))

    def next_block(work, source, target):
        inverse = columns_of(work, 8)

        def body(block, carry):
            value = zero
            for q in range(8):
                value = value + inverse[q] * row_of(source, block, q)
            put_block(target, block, value)
            return carry

        lax.fori_loop(0, nb, body, 0, unroll=2)

    basis = [current, previous]
    next_block(work, image, basis[0])
    coupling = None
    for step in range(STEPS):
        now, before = basis[step % 2], basis[(step + 1) % 2]

        def scale_block(block, carry):
            value = block_of(inv_root, block) * block_of(now, block)
            put_block(scaled, block, value)
            own[block] = value.astype(jnp.bfloat16)
            extended[step, block] = value.astype(jnp.bfloat16)
            return carry

        lax.fori_loop(0, nb, scale_block, 0, unroll=4)

        def gather_block(c, carry):
            for side in range(2):
                where = jnp.broadcast_to(bound_ref[pl.ds(side * nh + c, 1), :], (8, LANES))
                spot = jnp.bitwise_and(where, LANES - 1)
                source = jnp.right_shift(where, 7)
                found = zero
                for s in range(nb):
                    picked = jnp.take_along_axis(
                        scaled[s * 8 : s * 8 + 8, :], spot, axis=1, mode="promise_in_bounds"
                    )
                    found = jnp.where(source == s, picked, found)
                halo_send[step, side, c] = found.astype(jnp.bfloat16)
            return carry

        lax.fori_loop(0, nh, gather_block, 0)
        for copy in halo_copies(step):
            copy.start()
        col_products(lambda ref, t: own[ref[t]])
        send_returns(step + 1)
        for copy in halo_copies(step):
            copy.wait()
        row_products(lambda ref, t: extended[step, ref[t]])
        for copy in ret_copies(step + 1):
            copy.wait()

        def image_block(block, accs):
            root = block_of(inv_root, block)
            value = block_of(now, block)
            value = value - root * (root * value) - root * summed(step + 1, block)
            put_block(image, block, value)
            return tuple(accs[q] + value * row_of(now, block, q) for q in range(8))

        accs = lax.fori_loop(0, nb, image_block, (zero,) * 8)
        gram_begin(1 + 2 * step, fold(accs))
        alpha = gram_end(1 + 2 * step)
        alpha_ref[step] = alpha
        alpha_cols = columns_of(alpha, 0)
        coupling_cols = columns_of(coupling, 0) if step else None

        def residual_block(block, carry):
            value = block_of(image, block)
            for q in range(8):
                value = value - alpha_cols[q] * row_of(now, block, q)
            if step:
                for q in range(8):
                    value = value - coupling_cols[q] * row_of(before, block, q)
            put_block(image, block, value)
            return carry

        lax.fori_loop(0, nb, residual_block, 0, unroll=2)
        gram_begin(2 + 2 * step, gram_of(image, image))
        factor, work = factorise(gram_end(2 + 2 * step))
        beta_ref[step] = factor
        coupling = work
        next_block(work, image, before)

    last = basis[STEPS % 2]
    for p in range(probes_dev):
        for b in range(nb):
            basis_ref[p, pl.ds(b, 1), :] = last[pl.ds(b * 8 + my_probe * probes_dev + p, 1), :]


def order_of(keys, kinds, slots):
    index = jnp.arange(slots, dtype=jnp.int32)
    unique = keys * slots + index
    rank = jnp.sum((unique[None, :] < unique[:, None]).astype(jnp.int32), axis=1)
    placed = rank[:, None] == index[None, :]
    perm = jnp.sum(jnp.where(placed, index[:, None], 0), axis=0)
    sorted_keys = jnp.sum(jnp.where(placed, keys[:, None], 0), axis=0)
    keep = jnp.concatenate([jnp.zeros((1,), jnp.bool_), sorted_keys[1:] == sorted_keys[:-1]]).astype(jnp.float32)
    kind = jnp.arange(kinds, dtype=jnp.int32)
    up_to = jnp.sum((keys[None, :] <= kind[:, None]).astype(jnp.int32), axis=1)
    some = jnp.sum((keys[None, :] == kind[:, None]).astype(jnp.int32), axis=1)
    return perm, keep, jnp.where(some > 0, up_to - 1, slots)


def inverse_of(bound, nb):
    halo = bound.shape[1]
    h = jnp.arange(halo, dtype=jnp.int32)
    in_block = jnp.right_shift(bound, 7)[:, None, :] == jnp.arange(nb, dtype=jnp.int32)[None, :, None]
    at_lane = jnp.bitwise_and(bound, LANES - 1)[:, :, None] == jnp.arange(LANES, dtype=jnp.int32)[None, None, :]
    high = jnp.where(in_block, (jnp.right_shift(h, 6) + 1)[None, None, :], 0).astype(jnp.bfloat16)
    low = jnp.where(in_block, jnp.bitwise_and(h, 63)[None, None, :], 0).astype(jnp.bfloat16)
    both = jnp.einsum(
        "lbh,lhj->lbj", jnp.concatenate([high, low], axis=1), at_lane.astype(jnp.bfloat16),
        preferred_element_type=jnp.float32,
    ).astype(jnp.int32)
    return ((both[:, :nb] - 1) * 64 + both[:, nb:]).reshape(2 * nb, LANES)


def local(start_block, blocks, block_rows, block_cols, counts, boundary):
    n_rows, n_probe = lax.axis_size("rows"), lax.axis_size("probe")
    probes_dev, rows_dev = start_block.shape
    slots = blocks.shape[0]
    nb = rows_dev // LANES
    nh = nb // 2
    live = jnp.arange(slots, dtype=jnp.int32) < counts[0]
    perm_r, keep_r, end_r = order_of(jnp.where(live, block_rows, 2 * nb), nb, slots)
    perm_c, keep_c, end_c = order_of(jnp.where(live, block_cols, 2 * nb), 2 * nb, slots)
    inverse = inverse_of(boundary, nb)
    f32, bf16 = jnp.float32, jnp.bfloat16
    n_gram = 1 + 2 * STEPS
    vmem = pl.BlockSpec(memory_space=pltpu.VMEM)
    smem = pl.BlockSpec(memory_space=pltpu.SMEM)
    dma = pltpu.SemaphoreType.DMA
    basis, alpha, beta = pl.pallas_call(
        functools.partial(kernel, n_rows, n_probe, rows_dev * n_rows),
        out_shape=(
            jax.ShapeDtypeStruct((probes_dev, nb, LANES), f32),
            jax.ShapeDtypeStruct((STEPS, 8, LANES), f32),
            jax.ShapeDtypeStruct((STEPS, 8, LANES), f32),
        ),
        in_specs=[vmem, pl.BlockSpec(memory_space=pl.ANY)] + [smem] * 8 + [vmem, vmem],
        out_specs=(vmem, vmem, vmem),
        scratch_shapes=[
            pltpu.VMEM(blocks.shape, bf16),
            pltpu.VMEM((8, nb, LANES), f32),
            pltpu.VMEM((nb * 8, LANES), f32),
            pltpu.VMEM((nb * 8, LANES), f32),
            pltpu.VMEM((nb * 8, LANES), f32),
            pltpu.VMEM((nb * 8, LANES), f32),
            pltpu.VMEM((nb * 8, LANES), f32),
            pltpu.VMEM((nb, 8, LANES), bf16),
            pltpu.VMEM((STEPS, 2 * nb, 8, LANES), bf16),
            pltpu.VMEM((STEPS, 2, nh, 8, LANES), bf16),
            pltpu.VMEM((STEPS + 1, 2, nh, 8, LANES), f32),
            pltpu.VMEM((STEPS + 1, 2, nh, 8, LANES), f32),
            pltpu.VMEM((slots + 1, 8, LANES), f32),
            pltpu.VMEM((slots + 1, 8, LANES), f32),
            pltpu.VMEM((n_gram, 8, LANES), f32),
            pltpu.VMEM((n_gram, n_rows, 8, LANES), f32),
            dma,
            dma((n_probe,)),
            dma((n_probe,)),
            dma((STEPS, 2)),
            dma((STEPS, 2)),
            dma((STEPS + 1, 2)),
            dma((STEPS + 1, 2)),
            dma((n_gram, n_rows)),
            dma((n_gram, n_rows)),
        ],
        compiler_params=pltpu.CompilerParams(
            collective_id=0, has_side_effects=True, vmem_limit_bytes=48 * 1024 * 1024
        ),
        name="lanczos",
    )(
        start_block.reshape(probes_dev, nb, LANES), blocks, perm_r, keep_r, end_r, perm_c, keep_c, end_c,
        block_rows, block_cols, boundary.reshape(2 * nh, LANES), inverse,
    )
    return basis.reshape(probes_dev, rows_dev), alpha[:, :, :8], beta[:, :, :8]


def solution(mesh):
    in_specs = (
        P("probe", "rows"),
        P("rows", None, None),
        P("rows"),
        P("rows"),
        P("rows"),
        P(None, "rows"),
    )
    out_specs = (P("probe", "rows"), P(), P())
    return jax.shard_map(local, mesh=mesh, in_specs=in_specs, out_specs=out_specs, check_vma=False)
```

profile of v0, /device:TPU:0, one launch (start us, length us, event | category | flops | bytes accessed | tf_op | source)
XLA Modules:
  0.0 102.6 jit_solution(1031947519859170546)
XLA Ops:
  0.6 0.0 copy-start.2
  0.6 0.0 copy-start.1
  0.7 0.0 copy-start.3
  0.7 0.0 copy-start.4
  1.3 0.7 iota_add_fusion
  2.0 0.1 convert_reduce_fusion.2
  2.1 0.1 convert_reduce_fusion.4
  2.3 0.7 broadcast_shift-right-arithmetic_fusion
  3.0 0.1 select_convert_fusion.1
  3.1 1.0 fusion.1
  4.1 0.2 convert_reduce_fusion.1
  4.3 0.1 select_reduce_fusion.2
  4.4 0.1 slice_compare_fusion.1
  4.5 0.1 fusion.7.keep_r
  4.6 0.2 convert_reduce_fusion
  4.8 0.1 select_reduce_fusion
  4.9 0.1 slice_compare_fusion
  5.0 0.1 fusion.8.keep_c
  5.1 0.0 copy-done.4
  5.1 0.0 copy-done.3
  5.1 0.0 copy-done.2
  5.1 0.0 copy-done.1
  5.1 0.0 copy-start
  5.1 2.2 %copy-done = bf16[128,128,128]{2,1,0:T(8,128)(2,1)S(1)} copy-done((bf16[128,128,128]{2,1,0:T(8,128)(2,1)S(1)}, bf16[128,128,128]{2,1,0:T(8,128)(2,1)}, u32[]{:S(2)}) %copy-start) | copy-done | bytes 4194328
  7.3 93.5 %lanczos.1 = (f32[2,32,128]{2,1,0:T(8,128)S(1)}, f32[3,8,128]{2,1,0:T(8,128)S(1)}, f32[3,8,128]{2,1,0:T(8,128)S(1)}) custom-call(f32[2,32,128]{2,1,0:T(8,128)S(1)} %bitcast.14, bf16[128,128,128]{2,1,0:T(8,128)(2,1)S(1)} %copy-done, s32[128]{0:T(128)S(1)} %get-tuple-element.16.perm_r, f32[128]{0:T(128)S(1)} %fusion.7.keep_r, ...), custom_call_target="tpu_custom_call" | custom-call | tf_op jit(solution)/shard_map/lanczos/pallas_call | solution.py:383
  100.8 0.6 copy.13
  101.4 0.6 copy.18
  102.0 0.6 copy.19
  (6 shorter events, 0.0 us)
Async XLA Ops:
  0.6 4.5 %copy-start.2 = (s32[128]{0:T(128)S(1)}, s32[128]{0:T(128)}, u32[]{:S(2)}) copy-start(s32[128]{0:T(128)} %rows_ref.1) | copy-start | bytes 1540
  0.6 4.5 %copy-start.1 = (s32[128]{0:T(128)S(1)}, s32[128]{0:T(128)}, u32[]{:S(2)}) copy-start(s32[128]{0:T(128)} %cols_ref.1) | copy-start | bytes 1540
  0.7 4.4 %copy-start.3 = (s32[2,2048]{1,0:T(2,128)S(1)}, s32[2,2048]{1,0:T(2,128)}, u32[]{:S(2)}) copy-start(s32[2,2048]{1,0:T(2,128)} %param.11) | copy-start | bytes 49156
  0.7 4.4 %copy-start.4 = (f32[2,4096]{1,0:T(2,128)S(1)}, f32[2,4096]{1,0:T(2,128)}, u32[]{:S(2)}) copy-start(f32[2,4096]{1,0:T(2,128)} %param.6) | copy-start | bytes 98308
  5.1 2.2 %copy-start = (bf16[128,128,128]{2,1,0:T(8,128)(2,1)S(1)}, bf16[128,128,128]{2,1,0:T(8,128)(2,1)}, u32[]{:S(2)}) copy-start(bf16[128,128,128]{2,1,0:T(8,128)(2,1)} %tiles_hbm.1) | copy-start | bytes 12582916
where the time goes:
time: 103 us
  Pallas kernels  93.5 us (91%)
  local copies, waits for them, and re-layouts  4.06 us (4%)
  other arithmetic  2.65 us (3%)
  between operations  1.43 us (1%)
    pallas_call x1, Pallas kernels, local(): pl.pallas_call(functools.partial(kernel, n_rows, n_probe, rows_dev * n_ro...  93.5 us
    unnamed x14, local copies, waits for them, and re-layouts  4.04 us

commit v1 on v0

v1 whole, which is shorter than its diff:
```python
import functools

import jax
import jax.numpy as jnp
from jax import lax
from jax.experimental import pallas as pl
from jax.experimental.pallas import tpu as pltpu
from jax.sharding import PartitionSpec as P

STEPS = 3
LANES = 128
PLANES = 2
RETURN_TYPE = jnp.float32
MESH = pl.DeviceIdType.MESH
BY_COL, COL_OTHER, COL_END, COL_KEEP, BY_ROW, ROW_OTHER, ROW_END, ROW_KEEP = range(8)


def kernel(
    n_rows, n_probe, node_total,
    start_ref, tiles_hbm, rows_ref, cols_ref, counts_ref, bound_ref,
    basis_ref, coef_ref,
    tiles, gathered, vec, scaled, inv_root, inverse, table_v, table,
    own, extended_0, extended_1, extended_2, halo_send, ret_send, ret_recv, deg_send, deg_recv, row_sums, col_sums, gram_send, gram_recv,
    tile_sem, table_sem, start_send, start_recv, halo_ssem, halo_rsem, ret_ssem, ret_rsem, deg_ssem, deg_rsem,
    gram_ssem, gram_rsem,
):
    me = lax.axis_index("rows")
    my_probe = lax.axis_index("probe")
    slots = tiles.shape[0]
    nb = inv_root.shape[0]
    nh = nb // 2
    probes_dev = start_ref.shape[0]
    lower = lax.rem(me + n_rows - 1, n_rows)
    upper = lax.rem(me + 1, n_rows)
    f32, bf16 = jnp.float32, jnp.bfloat16
    extended = (extended_0, extended_1, extended_2)

    tile_copy = pltpu.make_async_copy(tiles_hbm, tiles, tile_sem)
    tile_copy.start()

    barrier = pltpu.get_barrier_semaphore()
    for off in range(1, n_probe):
        peer = lax.rem(my_probe + off, n_probe)
        pl.semaphore_signal(barrier, inc=1, device_id={"probe": peer}, device_id_type=MESH)

    def greet(off, carry):
        peer = lax.rem(me + off, n_rows)
        pl.semaphore_signal(barrier, inc=1, device_id={"rows": peer}, device_id_type=MESH)
        return carry

    lax.fori_loop(1, n_rows, greet, 0)

    lane = lax.broadcasted_iota(jnp.int32, (8, LANES), 1)
    sub = lax.broadcasted_iota(jnp.int32, (8, LANES), 0)
    zero = jnp.zeros((8, LANES), f32)

    lane_s = lax.broadcasted_iota(jnp.int32, (slots, slots), 1).astype(f32)
    sub_s = lax.broadcasted_iota(jnp.int32, (slots, slots), 0).astype(f32)
    lane_k = lax.broadcasted_iota(jnp.int32, (slots, LANES), 1).astype(f32)
    diagonal = lane_s == sub_s
    slot = lax.broadcasted_iota(jnp.int32, (1, slots), 1)
    live = slot < counts_ref[0]

    def down(row):
        return jnp.sum(jnp.where(diagonal, jnp.broadcast_to(row, (slots, slots)), 0.0), axis=1, keepdims=True)

    def order(keys, other, others_most, first):
        key = jnp.where(live, keys, 2 * nb).astype(f32)
        key_down = down(key)
        other_down = down(other.astype(f32))
        key_row = jnp.broadcast_to(key, (slots, slots))
        same = key_row == key_down
        before = jnp.where(same, jnp.where(lane_s < sub_s, 1.0, 0.0), 0.0)
        rank = jnp.sum(jnp.where(key_row < key_down, 1.0, before), axis=1, keepdims=True)
        kept = jnp.where(jnp.sum(before, axis=1, keepdims=True) > 0.0, 1.0, 0.0)
        placed = rank == lane_s
        perm = jnp.sum(jnp.where(placed, sub_s, 0.0), axis=0, keepdims=True)
        others = jnp.sum(jnp.where(placed, other_down, 0.0), axis=0, keepdims=True)
        keep = jnp.sum(jnp.where(placed, kept, 0.0), axis=0, keepdims=True)
        up_to = jnp.sum(jnp.where(key_down <= lane_k, 1.0, 0.0), axis=0, keepdims=True)
        some = jnp.sum(jnp.where(key_down == lane_k, 1.0, 0.0), axis=0, keepdims=True)
        end = jnp.where(some > 0.0, up_to - 1.0, float(slots))
        rows = ((perm, slots - 1), (others, others_most), (end, slots), (keep, 1))
        for place, (value, most) in enumerate(rows):
            table_v[first + place : first + place + 1, :] = jnp.clip(value.astype(jnp.int32), 0, most)

    order(cols_ref[...], rows_ref[...], nb - 1, BY_COL)
    order(rows_ref[...], cols_ref[...], 2 * nb - 1, BY_ROW)
    table_copy = pltpu.make_async_copy(table_v, table, table_sem)
    table_copy.start()

    pl.semaphore_wait(barrier, n_probe - 1 + n_rows - 1)

    def start_copy(off):
        peer = lax.rem(my_probe + off, n_probe)
        return pltpu.make_async_remote_copy(
            src_ref=start_ref,
            dst_ref=gathered.at[my_probe],
            send_sem=start_send.at[off],
            recv_sem=start_recv.at[off],
            device_id={"probe": peer},
            device_id_type=MESH,
        )

    for off in range(1, n_probe):
        start_copy(off).start()
    gathered[my_probe] = start_ref[...]
    table_copy.wait()

    def row_of(k, block, probe):
        return jnp.broadcast_to(vec[k, pl.ds(block * 8 + probe, 1), :], (8, LANES))

    def block_of(k, block):
        return vec[k, pl.ds(pl.multiple_of(block * 8, 8), 8), :]

    def put_block(k, block, value):
        vec[k, pl.ds(pl.multiple_of(block * 8, 8), 8), :] = value

    def root_of(block):
        return jnp.broadcast_to(inv_root[pl.ds(block, 1), :], (8, LANES))

    def gram_copy(index, off):
        peer = lax.rem(me + off, n_rows)
        return pltpu.make_async_remote_copy(
            src_ref=gram_send.at[index],
            dst_ref=gram_recv.at[index, me],
            send_sem=gram_ssem.at[index, off],
            recv_sem=gram_rsem.at[index, off],
            device_id={"rows": peer},
            device_id_type=MESH,
        )

    def gram_begin(index, accs):
        gram = zero
        for q, acc in enumerate(accs):
            gram = jnp.where(lane == q, jnp.sum(acc, axis=1, keepdims=True), gram)
        gram_send[index] = gram
        gram_recv[index, me] = gram

        def send(off, carry):
            gram_copy(index, off).start()
            return carry

        lax.fori_loop(1, n_rows, send, 0)

    def gram_end(index, count):
        def wait(off, carry):
            gram_copy(index, off).wait()
            return carry

        lax.fori_loop(1, n_rows, wait, 0)
        gram = jnp.sum(gram_recv[index], axis=0) * (1.0 / node_total)
        return [jnp.broadcast_to(gram[:, q : q + 1], (8, LANES)) for q in range(count)]

    def grams(pairs):
        def body(block, accs):
            out = []
            for i, (left, right) in enumerate(pairs):
                value = block_of(left, block)
                out += [accs[i * 8 + q] + value * row_of(right, block, q) for q in range(8)]
            return tuple(out)

        return lax.fori_loop(0, nb, body, (zero,) * (8 * len(pairs)), unroll=8)

    def spread(column, row):
        return jnp.broadcast_to(column[row : row + 1, :], (8, LANES))

    def factorise(work):
        work = list(work)
        inverse_cols = [jnp.where(sub == q, 1.0, 0.0) for q in range(8)]
        factor = []
        scale = zero
        for j in range(8):
            root = lax.rsqrt(spread(work[j], j))
            scale = jnp.where(sub == j, root, scale)
            part = work[j] * root
            factor.append(jnp.where(sub >= j, part, 0.0))
            lower_part = jnp.where(sub > j, part * root, 0.0)
            for q in range(j + 1, 8):
                work[q] = work[q] - lower_part * spread(work[q], j)
            for q in range(j + 1):
                inverse_cols[q] = inverse_cols[q] - lower_part * spread(inverse_cols[q], j)
        inverse_cols = [column * scale for column in inverse_cols]
        transposed = [jnp.where(sub <= q, work[q] * scale, 0.0) for q in range(8)]
        return factor, inverse_cols, transposed

    def product(left, right):
        out = []
        for q in range(8):
            value = left[0] * spread(right[q], 0)
            for k in range(1, 8):
                value = value + left[k] * spread(right[q], k)
            out.append(value)
        return out

    def outer(left):
        out = []
        for q in range(8):
            value = left[0] * spread(left[0], q)
            for k in range(1, 8):
                value = value + left[k] * spread(left[k], q)
            out.append(value)
        return out

    def minus(left, right):
        return [a - b for a, b in zip(left, right)]

    def put_matrix(place, columns):
        value = zero
        for q in range(8):
            value = jnp.where(lane == q, columns[q], value)
        coef_ref[place] = value

    def mixed(terms, block):
        value = None
        for columns, k in terms:
            for q in range(8):
                part = columns[q] * row_of(k, block, q)
                value = part if value is None else value + part
        return value

    def mix(terms, target):
        def body(block, carry):
            put_block(target, block, mixed(terms, block))
            return carry

        lax.fori_loop(0, nb, body, 0, unroll=4)

    def folded(value):
        return value if value.shape[0] == 8 else value[:8] + value[8:]

    def col_products(lhs_of):
        def body(m, acc):
            y = jnp.dot(lhs_of(table[COL_OTHER, m]), tiles[table[BY_COL, m]], preferred_element_type=f32)
            acc = acc * table[COL_KEEP, m].astype(f32) + folded(y)
            col_sums[m] = acc
            return acc

        lax.fori_loop(0, slots, body, zero, unroll=64)

    def row_products(lhs_of):
        def body(m, acc):
            y = lax.dot_general(
                lhs_of(table[ROW_OTHER, m]), tiles[table[BY_ROW, m]], (((1,), (1,)), ((), ())),
                preferred_element_type=f32,
            )
            acc = acc * table[ROW_KEEP, m].astype(f32) + folded(y)
            row_sums[m] = acc
            return acc

        lax.fori_loop(0, slots, body, zero, unroll=64)

    row_sums[slots] = zero
    col_sums[slots] = zero

    def exchange(src, dst, ssem, rsem):
        return [
            pltpu.make_async_remote_copy(
                src_ref=src(side),
                dst_ref=dst(1 - side),
                send_sem=ssem(side),
                recv_sem=rsem(side),
                device_id={"rows": lower if side == 0 else upper},
                device_id_type=MESH,
            )
            for side in range(2)
        ]

    tile_copy.wait()
    ones = jnp.ones((8, LANES), bf16)
    col_products(lambda b: ones)
    for side in range(2):
        for c in range(nh):
            deg_send[side, c : c + 1, :] = col_sums[table[COL_END, nb + side * nh + c], 0:1, :]
    deg_copies = exchange(
        lambda side: deg_send.at[side], lambda side: deg_recv.at[side],
        lambda side: deg_ssem.at[side], lambda side: deg_rsem.at[side],
    )
    for copy in deg_copies:
        copy.start()

    for off in range(1, n_probe):
        start_copy(off).wait()

    def take_start(block, carry):
        where = pl.ds(pl.multiple_of(block * LANES, LANES), LANES)
        for g in range(n_probe):
            vec[0, pl.ds(block * 8 + g * probes_dev, probes_dev), :] = gathered[g, :, where]
        return carry

    lax.fori_loop(0, nb, take_start, 0, unroll=8)
    gram_begin(0, grams([(0, 0)]))

    row_products(lambda b: ones)

    sub_l = lax.broadcasted_iota(jnp.int32, (LANES, LANES), 0)
    sub_b = lax.broadcasted_iota(jnp.int32, (nb, LANES), 0)
    lane_b = lax.broadcasted_iota(jnp.int32, (nb, LANES), 1)
    for side in range(2):
        total = jnp.zeros((2 * nb, LANES), f32)
        for c in range(nh):
            where = bound_ref[side : side + 1, c * LANES : (c + 1) * LANES]
            in_block = sub_b == jnp.broadcast_to(jnp.right_shift(where, 7), (nb, LANES))
            at_lane = sub_l == jnp.broadcast_to(jnp.bitwise_and(where, LANES - 1), (LANES, LANES))
            h = lane_b + c * LANES
            high = jnp.where(in_block, (jnp.right_shift(h, 6) + 1).astype(f32), 0.0)
            low = jnp.where(in_block, jnp.bitwise_and(h, 63).astype(f32), 0.0)
            total = total + lax.dot_general(
                jnp.concatenate([high, low], axis=0).astype(bf16), jnp.where(at_lane, 1.0, 0.0).astype(bf16),
                (((1,), (1,)), ((), ())), preferred_element_type=f32,
            )
        inverse[pl.ds(side * nb, nb), :] = ((total[:nb] - 1.0) * 64.0 + total[nb:]).astype(jnp.int32)

    def found_of(source_of, where, count, kind):
        spot = jnp.bitwise_and(where, LANES - 1)
        block = jnp.right_shift(where, 7)
        found = zero
        for s in range(count):
            picked = jnp.take_along_axis(source_of(s).astype(f32), spot, axis=1, mode="promise_in_bounds")
            found = jnp.where(block == s, picked, found)
        return found

    for b in range(nb):
        inv_root[b : b + 1, :] = row_sums[table[ROW_END, b], 0:1, :] + col_sums[table[COL_END, b], 0:1, :]
    for copy in deg_copies:
        copy.wait()
    for g in range(nb // 8):
        degree = 1.0 + inv_root[g * 8 : g * 8 + 8, :]
        for side in range(2):
            degree = degree + found_of(
                lambda s: jnp.broadcast_to(deg_recv[side, s : s + 1, :], (8, LANES)),
                inverse[side * nb + g * 8 : side * nb + g * 8 + 8, :], nh, f32,
            )
        inv_root[g * 8 : g * 8 + 8, :] = 1.0 / jnp.sqrt(degree)

    def planes(value):
        top = value.astype(bf16)
        if PLANES == 1:
            return top
        return jnp.concatenate([top, (value - top.astype(f32)).astype(bf16)], axis=0)

    def scale_block(step, block, value):
        value = root_of(block) * value
        scaled[pl.ds(pl.multiple_of(block * 8, 8), 8), :] = value
        pieces = planes(value)
        own[block] = pieces
        extended[step][block] = pieces

    def send_halo(step):
        def gather_block(c, carry):
            for side in range(2):
                piece = bound_ref[side : side + 1, pl.ds(pl.multiple_of(c * LANES, LANES), LANES)]
                found = found_of(
                    lambda s: scaled[s * 8 : s * 8 + 8, :], jnp.broadcast_to(piece, (8, LANES)), nb, f32
                )
                halo_send[step, side, c] = planes(found)
            return carry

        lax.fori_loop(0, nh, gather_block, 0, unroll=2)
        copies = exchange(
            lambda side: halo_send.at[step, side], lambda side: extended[step].at[pl.ds(nb + side * nh, nh)],
            lambda side: halo_ssem.at[step, side], lambda side: halo_rsem.at[step, side],
        )
        for copy in copies:
            copy.start()
        return copies

    def send_returns(step):
        col_products(lambda b: own[b])
        for side in range(2):
            for c in range(nh):
                ret_send[step, side, c] = col_sums[table[COL_END, nb + side * nh + c]].astype(RETURN_TYPE)
        copies = exchange(
            lambda side: ret_send.at[step, side], lambda side: ret_recv.at[step, side],
            lambda side: ret_ssem.at[step, side], lambda side: ret_rsem.at[step, side],
        )
        for copy in copies:
            copy.start()
        return copies

    def combine(step, source, target):
        def body(block, carry):
            total = row_sums[table[ROW_END, block]] + col_sums[table[COL_END, block]]
            for side in range(2):
                where = jnp.broadcast_to(inverse[pl.ds(side * nb + block, 1), :], (8, LANES))
                total = total + found_of(lambda s: ret_recv[step, side, s], where, nh, f32)
            root = root_of(block)
            put_block(target, block, -(root * (root * block_of(source, block) + total)))
            return carry

        lax.fori_loop(0, nb, body, 0, unroll=4)

    start_at, image_at = 0, STEPS + 4

    def q_at(j):
        return j

    def u_at(j):
        return STEPS + j

    coupling = None
    for step in range(STEPS):
        source = start_at if step == 0 else u_at(step)

        if step == 0:
            def body(block, carry):
                scale_block(0, block, block_of(start_at, block))
                return carry

            lax.fori_loop(0, nb, body, 0, unroll=4)
        halos = send_halo(step)
        returns = send_returns(step)
        if step:
            mix(q_terms, q_at(step))
            gram_begin(step, grams([(u_at(step), u_at(step)), (u_at(step), q_at(step))]))
        for copy in halos:
            copy.wait()
        row_products(lambda b: extended[step][b])

        if step == 0:
            factor, inv_cols, next_coupling = factorise(gram_end(0, 8))
            q_terms = [(inv_cols, start_at)]
            u_terms = [(inv_cols, image_at)]
        else:
            gram = gram_end(step, 16)
            shift = gram[8:]
            rest = minus(gram[:8], outer(shift))
            if step > 1:
                rest = minus(rest, outer(coupling))
            factor, inv_cols, next_coupling = factorise(rest)
            put_matrix(step - 1, [column + jnp.where(sub == q, 1.0, 0.0) for q, column in enumerate(shift)])
            put_matrix(STEPS + step - 1, factor)
            less = [-column for column in product(inv_cols, shift)]
            q_terms = [(inv_cols, u_at(step)), (less, q_at(step))]
            u_terms = [(inv_cols, image_at), (less, u_at(step))]
            if step > 1:
                less = [-column for column in product(inv_cols, coupling)]
                q_terms.append((less, q_at(step - 1)))
                u_terms.append((less, u_at(step - 1)))
        coupling = next_coupling

        for copy in returns:
            copy.wait()
        combine(step, source, image_at)

        def next_image(block, carry):
            value = mixed(u_terms, block)
            put_block(u_at(step + 1), block, value)
            if step + 1 < STEPS:
                scale_block(step + 1, block, value)
            return carry

        lax.fori_loop(0, nb, next_image, 0, unroll=4)

    mix(q_terms, q_at(STEPS))
    gram_begin(STEPS, grams([(u_at(STEPS), u_at(STEPS)), (u_at(STEPS), q_at(STEPS))]))
    gram = gram_end(STEPS, 16)
    shift = gram[8:]
    rest = minus(minus(gram[:8], outer(shift)), outer(coupling))
    factor, inv_cols, _ = factorise(rest)
    put_matrix(STEPS - 1, [column + jnp.where(sub == q, 1.0, 0.0) for q, column in enumerate(shift)])
    put_matrix(2 * STEPS - 1, factor)
    q_terms = [
        (inv_cols, u_at(STEPS)),
        ([-column for column in product(inv_cols, shift)], q_at(STEPS)),
        ([-column for column in product(inv_cols, coupling)], q_at(STEPS - 1)),
    ]
    mix(q_terms, start_at)
    for p in range(probes_dev):
        for b in range(nb):
            basis_ref[p : p + 1, b * LANES : (b + 1) * LANES] = vec[
                start_at, pl.ds(b * 8 + my_probe * probes_dev + p, 1), :
            ]


def local(start_block, blocks, block_rows, block_cols, counts, boundary):
    n_rows, n_probe = lax.axis_size("rows"), lax.axis_size("probe")
    probes_dev, rows_dev = start_block.shape
    slots = blocks.shape[0]
    nb = rows_dev // LANES
    nh = nb // 2
    f32, bf16 = jnp.float32, jnp.bfloat16
    vmem = pl.BlockSpec(memory_space=pltpu.VMEM)
    smem = pl.BlockSpec(memory_space=pltpu.SMEM)
    dma = pltpu.SemaphoreType.DMA
    height = 8 * PLANES
    basis, coef = pl.pallas_call(
        functools.partial(kernel, n_rows, n_probe, rows_dev * n_rows),
        out_shape=(
            jax.ShapeDtypeStruct((probes_dev, rows_dev), f32),
            jax.ShapeDtypeStruct((2 * STEPS, 8, LANES), f32),
        ),
        in_specs=[vmem, pl.BlockSpec(memory_space=pltpu.HBM), vmem, vmem, smem, vmem],
        out_specs=(vmem, vmem),
        scratch_shapes=[
            pltpu.VMEM(blocks.shape, bf16),
            pltpu.VMEM((n_probe, probes_dev, rows_dev), f32),
            pltpu.VMEM((2 * STEPS + 2, nb * 8, LANES), f32),
            pltpu.VMEM((nb * 8, LANES), f32),
            pltpu.VMEM((nb, LANES), f32),
            pltpu.VMEM((2 * nb, LANES), jnp.int32),
            pltpu.VMEM((8, LANES), jnp.int32),
            pltpu.SMEM((8, LANES), jnp.int32),
            pltpu.VMEM((nb, height, LANES), bf16),
            *[pltpu.VMEM((2 * nb, height, LANES), bf16)] * STEPS,
            pltpu.VMEM((STEPS, 2, nh, height, LANES), bf16),
            pltpu.VMEM((STEPS, 2, nh, 8, LANES), RETURN_TYPE),
            pltpu.VMEM((STEPS, 2, nh, 8, LANES), RETURN_TYPE),
            pltpu.VMEM((2, nh, LANES), f32),
            pltpu.VMEM((2, nh, LANES), f32),
            pltpu.VMEM((slots + 1, 8, LANES), f32),
            pltpu.VMEM((slots + 1, 8, LANES), f32),
            pltpu.VMEM((STEPS + 1, 8, LANES), f32),
            pltpu.VMEM((STEPS + 1, n_rows, 8, LANES), f32),
            dma,
            dma,
            dma((n_probe,)),
            dma((n_probe,)),
            dma((STEPS, 2)),
            dma((STEPS, 2)),
            dma((STEPS, 2)),
            dma((STEPS, 2)),
            dma((2,)),
            dma((2,)),
            dma((STEPS + 1, n_rows)),
            dma((STEPS + 1, n_rows)),
        ],
        compiler_params=pltpu.CompilerParams(
            collective_id=0, has_side_effects=True, vmem_limit_bytes=48 * 1024 * 1024
        ),
        name="lanczos",
    )(
        start_block, blocks, block_rows.reshape(1, slots), block_cols.reshape(1, slots), counts, boundary,
    )
    return basis, coef[:STEPS, :, :8], coef[STEPS:, :, :8]


def solution(mesh):
    in_specs = (
        P("probe", "rows"),
        P("rows", None, None),
        P("rows"),
        P("rows"),
        P("rows"),
        P(None, "rows"),
    )
    out_specs = (P("probe", "rows"), P(), P())
    return jax.shard_map(local, mesh=mesh, in_specs=in_specs, out_specs=out_specs, check_vma=False)
```

time: 103 us -> 65.3 us (0.63)
  Pallas kernels: 93.5 us -> 57.5 us
  other arithmetic: 2.65 us -> 0 us
  local copies, waits for them, and re-layouts: 4.06 us -> 6.19 us
    pallas_call x1, Pallas kernels: 93.5 us -> 57.5 us  [local(): pl.pallas_call(functools.partial(kernel, n_rows, n_probe, rows_dev * n_ro...]
    unnamed x14 -> x11, local copies, waits for them, and re-layouts: 4.04 us -> 5.58 us
where the time goes in v1:
time: 65.3 us; the launch traced here: 65 us
  Pallas kernels  57.5 us (88%)
  local copies, waits for them, and re-layouts  6.19 us (9%)
  between operations  1.3 us (2%)
    pallas_call x1, Pallas kernels, local(): pl.pallas_call(functools.partial(kernel, n_rows, n_probe, rows_dev * n_ro...  57.5 us
    unnamed x11, local copies, waits for them, and re-layouts  5.58 us

profile of v1, /device:TPU:0, one launch (start us, length us, event | category | flops | bytes accessed | tf_op | source)
XLA Modules:
  0.0 65.0 jit_solution(3738141656193042214)
XLA Ops:
  1.3 0.0 copy-start
  1.3 2.2 %copy-done = bf16[128,128,128]{2,1,0:T(8,128)(2,1)S(1)} copy-done((bf16[128,128,128]{2,1,0:T(8,128)(2,1)S(1)}, bf16[128,128,128]{2,1,0:T(8,128)(2,1)}, u32[]{:S(2)}) %copy-start) | copy-done | bytes 4194328
  3.5 0.0 copy-start.1
  3.5 0.8 %copy-done.1 = f32[2,4096]{1,0:T(2,128)S(1)} copy-done((f32[2,4096]{1,0:T(2,128)S(1)}, f32[2,4096]{1,0:T(2,128)}, u32[]{:S(2)}) %copy-start.1) | copy-done | bytes 32792
  4.2 0.0 copy-start.2
  4.2 0.7 %copy-done.2 = s32[2,2048]{1,0:T(2,128)S(1)} copy-done((s32[2,2048]{1,0:T(2,128)S(1)}, s32[2,2048]{1,0:T(2,128)}, u32[]{:S(2)}) %copy-start.2) | copy-done | bytes 16408
  4.9 0.0 copy-start.3
  4.9 0.7 %copy-done.3 = s32[128]{0:T(128)S(1)} copy-done((s32[128]{0:T(128)S(1)}, s32[128]{0:T(128)}, u32[]{:S(2)}) %copy-start.3) | copy-done | bytes 536
  5.6 0.0 copy-start.4
  5.6 0.7 %copy-done.4 = s32[128]{0:T(128)S(1)} copy-done((s32[128]{0:T(128)S(1)}, s32[128]{0:T(128)}, u32[]{:S(2)}) %copy-start.4) | copy-done | bytes 536
  6.3 57.5 %lanczos.1 = (f32[2,4096]{1,0:T(2,128)S(1)}, f32[6,8,128]{2,1,0:T(8,128)S(1)}) custom-call(f32[2,4096]{1,0:T(2,128)S(1)} %copy-done.1, bf16[128,128,128]{2,1,0:T(8,128)(2,1)S(1)} %copy-done, s32[1,128]{1,0:T(1,128)S(1)} %bitcast.2, s32[1,128]{1,0:T(1,128)S(1)} %bitcast.3, s32[1]{0:T(128)S(6)} %copy.10.counts_ref, s32[2,2048]{1,0:T(2,128)S(1)} %copy-done.2), custom_call_target="tpu_custom_call" | custom-call | tf_op jit(solution)/shard_map/lanczos/pallas_call | solution.py:487
  63.8 0.6 fusion
  64.4 0.6 copy.11
Async XLA Ops:
  1.3 2.2 %copy-start = (bf16[128,128,128]{2,1,0:T(8,128)(2,1)S(1)}, bf16[128,128,128]{2,1,0:T(8,128)(2,1)}, u32[]{:S(2)}) copy-start(bf16[128,128,128]{2,1,0:T(8,128)(2,1)} %tiles_hbm.1) | copy-start | bytes 12582916
  3.5 0.8 %copy-start.1 = (f32[2,4096]{1,0:T(2,128)S(1)}, f32[2,4096]{1,0:T(2,128)}, u32[]{:S(2)}) copy-start(f32[2,4096]{1,0:T(2,128)} %start_ref.1) | copy-start | bytes 98308
  4.2 0.7 %copy-start.2 = (s32[2,2048]{1,0:T(2,128)S(1)}, s32[2,2048]{1,0:T(2,128)}, u32[]{:S(2)}) copy-start(s32[2,2048]{1,0:T(2,128)} %bound_ref.1) | copy-start | bytes 49156
  4.9 0.7 %copy-start.3 = (s32[128]{0:T(128)S(1)}, s32[128]{0:T(128)}, u32[]{:S(2)}) copy-start(s32[128]{0:T(128)} %param.8) | copy-start | bytes 1540
  5.6 0.7 %copy-start.4 = (s32[128]{0:T(128)S(1)}, s32[128]{0:T(128)}, u32[]{:S(2)}) copy-start(s32[128]{0:T(128)} %param.9) | copy-start | bytes 1540

commit v2 on v1

--- a/solution.py
+++ b/solution.py
@@ -10,6 +10,8 @@
 STEPS = 3
 LANES = 128
 PLANES = 2
+PIECES = 4
+VMEM_BYTES = 48 * 1024 * 1024
 RETURN_TYPE = jnp.float32
 MESH = pl.DeviceIdType.MESH
 BY_COL, COL_OTHER, COL_END, COL_KEEP, BY_ROW, ROW_OTHER, ROW_END, ROW_KEEP = range(8)
@@ -17,11 +19,11 @@
 
 def kernel(
     n_rows, n_probe, node_total,
-    start_ref, tiles_hbm, rows_ref, cols_ref, counts_ref, bound_ref,
+    start_hbm, tiles_hbm, rows_hbm, cols_hbm, counts_hbm, bound_hbm,
     basis_ref, coef_ref,
-    tiles, gathered, vec, scaled, inv_root, inverse, table_v, table,
-    own, extended_0, extended_1, extended_2, halo_send, ret_send, ret_recv, deg_send, deg_recv, row_sums, col_sums, gram_send, gram_recv,
-    tile_sem, table_sem, start_send, start_recv, halo_ssem, halo_rsem, ret_ssem, ret_rsem, deg_ssem, deg_rsem,
+    start_ref, tiles, turned, rows_ref, cols_ref, counts_ref, bound_ref, gathered, vec, scaled, inv_root, inverse, table_v, table,
+    own, extended_0, extended_1, extended_2, halo_send, ret_send, ret_recv, deg_send, deg_recv, part_send, part_recv, row_sums, col_sums, gram_send, gram_recv,
+    load_sem, table_sem, start_send, start_recv, halo_ssem, halo_rsem, ret_ssem, ret_rsem, part_ssem, part_rsem, deg_ssem, deg_rsem,
     gram_ssem, gram_rsem,
 ):
     me = lax.axis_index("rows")
@@ -32,11 +34,24 @@
     probes_dev = start_ref.shape[0]
     lower = lax.rem(me + n_rows - 1, n_rows)
     upper = lax.rem(me + 1, n_rows)
+    half = lax.rem(my_probe, 2)
+    sibling = my_probe + 1 - 2 * half
+    served = 1 - lax.rem(me + half, 2)
+    partner = lax.rem(me + 2 * served - 1 + n_rows, n_rows)
     f32, bf16 = jnp.float32, jnp.bfloat16
     extended = (extended_0, extended_1, extended_2)
 
-    tile_copy = pltpu.make_async_copy(tiles_hbm, tiles, tile_sem)
-    tile_copy.start()
+    loads = [
+        pltpu.make_async_copy(source, target, load_sem.at[i])
+        for i, (source, target) in enumerate(
+            (
+                (rows_hbm, rows_ref), (cols_hbm, cols_ref), (counts_hbm, counts_ref), (start_hbm, start_ref),
+                (bound_hbm, bound_ref), (tiles_hbm, tiles),
+            )
+        )
+    ]
+    for load in loads:
+        load.start()
 
     barrier = pltpu.get_barrier_semaphore()
     for off in range(1, n_probe):
@@ -59,6 +74,8 @@
     lane_k = lax.broadcasted_iota(jnp.int32, (slots, LANES), 1).astype(f32)
     diagonal = lane_s == sub_s
     slot = lax.broadcasted_iota(jnp.int32, (1, slots), 1)
+    for load in loads[:3]:
+        load.wait()
     live = slot < counts_ref[0]
 
     def down(row):
@@ -102,6 +119,7 @@
             device_id_type=MESH,
         )
 
+    loads[3].wait()
     for off in range(1, n_probe):
         start_copy(off).start()
     gathered[my_probe] = start_ref[...]
@@ -229,26 +247,23 @@
     def folded(value):
         return value if value.shape[0] == 8 else value[:8] + value[8:]
 
-    def col_products(lhs_of):
-        def body(m, acc):
-            y = jnp.dot(lhs_of(table[COL_OTHER, m]), tiles[table[BY_COL, m]], preferred_element_type=f32)
-            acc = acc * table[COL_KEEP, m].astype(f32) + folded(y)
-            col_sums[m] = acc
-            return acc
-
-        lax.fori_loop(0, slots, body, zero, unroll=64)
-
-    def row_products(lhs_of):
-        def body(m, acc):
+    def products(lhs_of, source, sums, first):
+        by, other, keep = first + BY_COL, first + COL_OTHER, first + COL_KEEP
+        acc = zero
+        for m in range(0, slots, 2):
+            pair = (m, m + 1)
+            lhs = [lhs_of(table[other, k]) for k in pair]
+            height = lhs[0].shape[0]
             y = lax.dot_general(
-                lhs_of(table[ROW_OTHER, m]), tiles[table[BY_ROW, m]], (((1,), (1,)), ((), ())),
+                jnp.concatenate(lhs, axis=0),
+                jnp.concatenate([source[table[by, k]] for k in pair], axis=1),
+                (((1,), (0,)), ((), ())),
                 preferred_element_type=f32,
             )
-            acc = acc * table[ROW_KEEP, m].astype(f32) + folded(y)
-            row_sums[m] = acc
-            return acc
-
-        lax.fori_loop(0, slots, body, zero, unroll=64)
+            for i, k in enumerate(pair):
+                part = y[i * height : (i + 1) * height, i * LANES : (i + 1) * LANES]
+                acc = acc * table[keep, k].astype(f32) + folded(part)
+                sums[k] = acc
 
     row_sums[slots] = zero
     col_sums[slots] = zero
@@ -266,9 +281,10 @@
             for side in range(2)
         ]
 
-    tile_copy.wait()
-    ones = jnp.ones((8, LANES), bf16)
-    col_products(lambda b: ones)
+    loads[4].wait()
+    loads[5].wait()
+    ones = jnp.concatenate([jnp.ones((8, LANES), bf16), jnp.zeros((8, LANES), bf16)], axis=0)
+    products(lambda b: ones, tiles, col_sums, BY_COL)
     for side in range(2):
         for c in range(nh):
             deg_send[side, c : c + 1, :] = col_sums[table[COL_END, nb + side * nh + c], 0:1, :]
@@ -279,19 +295,13 @@
     for copy in deg_copies:
         copy.start()
 
-    for off in range(1, n_probe):
-        start_copy(off).wait()
-
-    def take_start(block, carry):
-        where = pl.ds(pl.multiple_of(block * LANES, LANES), LANES)
-        for g in range(n_probe):
-            vec[0, pl.ds(block * 8 + g * probes_dev, probes_dev), :] = gathered[g, :, where]
+
+    def turn(t, carry):
+        turned[t] = tiles[t].T
         return carry
 
-    lax.fori_loop(0, nb, take_start, 0, unroll=8)
-    gram_begin(0, grams([(0, 0)]))
-
-    row_products(lambda b: ones)
+    lax.fori_loop(0, slots, turn, 0, unroll=16)
+    products(lambda b: ones, turned, row_sums, BY_ROW)
 
     sub_l = lax.broadcasted_iota(jnp.int32, (LANES, LANES), 0)
     sub_b = lax.broadcasted_iota(jnp.int32, (nb, LANES), 0)
@@ -311,7 +321,7 @@
             )
         inverse[pl.ds(side * nb, nb), :] = ((total[:nb] - 1.0) * 64.0 + total[nb:]).astype(jnp.int32)
 
-    def found_of(source_of, where, count, kind):
+    def found_of(source_of, where, count):
         spot = jnp.bitwise_and(where, LANES - 1)
         block = jnp.right_shift(where, 7)
         found = zero
@@ -320,6 +330,17 @@
             found = jnp.where(block == s, picked, found)
         return found
 
+    for off in range(1, n_probe):
+        start_copy(off).wait()
+
+    def take_start(block, carry):
+        where = pl.ds(pl.multiple_of(block * LANES, LANES), LANES)
+        for g in range(n_probe):
+            vec[0, pl.ds(block * 8 + g * probes_dev, probes_dev), :] = gathered[g, :, where]
+        return carry
+
+    lax.fori_loop(0, nb, take_start, 0, unroll=8)
+    gram_begin(0, grams([(0, 0)]))
     for b in range(nb):
         inv_root[b : b + 1, :] = row_sums[table[ROW_END, b], 0:1, :] + col_sums[table[COL_END, b], 0:1, :]
     for copy in deg_copies:
@@ -329,9 +350,10 @@
         for side in range(2):
             degree = degree + found_of(
                 lambda s: jnp.broadcast_to(deg_recv[side, s : s + 1, :], (8, LANES)),
-                inverse[side * nb + g * 8 : side * nb + g * 8 + 8, :], nh, f32,
+                inverse[side * nb + g * 8 : side * nb + g * 8 + 8, :], nh,
             )
         inv_root[g * 8 : g * 8 + 8, :] = 1.0 / jnp.sqrt(degree)
+
 
     def planes(value):
         top = value.astype(bf16)
@@ -339,58 +361,70 @@
             return top
         return jnp.concatenate([top, (value - top.astype(f32)).astype(bf16)], axis=0)
 
+    mine = (1 - half).astype(f32)
+
     def scale_block(step, block, value):
         value = root_of(block) * value
         scaled[pl.ds(pl.multiple_of(block * 8, 8), 8), :] = value
-        pieces = planes(value)
-        own[block] = pieces
-        extended[step][block] = pieces
+        own[block] = planes(value)
+        extended[step][block] = planes(value * mine)
+
+    for step in range(STEPS):
+        for c in range(nh):
+            extended[step][nb + (1 - served) * nh + c] = jnp.zeros((8 * PLANES, LANES), bf16)
+
+    def to_partner(src_ref, dst_ref, send_sem, recv_sem):
+        copy = pltpu.make_async_remote_copy(
+            src_ref=src_ref, dst_ref=dst_ref, send_sem=send_sem, recv_sem=recv_sem,
+            device_id={"rows": partner}, device_id_type=MESH,
+        )
+        copy.start()
+        return copy
 
     def send_halo(step):
         def gather_block(c, carry):
-            for side in range(2):
-                piece = bound_ref[side : side + 1, pl.ds(pl.multiple_of(c * LANES, LANES), LANES)]
-                found = found_of(
-                    lambda s: scaled[s * 8 : s * 8 + 8, :], jnp.broadcast_to(piece, (8, LANES)), nb, f32
-                )
-                halo_send[step, side, c] = planes(found)
+            where = pl.ds(pl.multiple_of(c * LANES, LANES), LANES)
+            piece = jnp.where(served == 1, bound_ref[1:2, where], bound_ref[0:1, where])
+            found = found_of(lambda s: scaled[s * 8 : s * 8 + 8, :], jnp.broadcast_to(piece, (8, LANES)), nb)
+            halo_send[step, c] = planes(found)
             return carry
 
-        lax.fori_loop(0, nh, gather_block, 0, unroll=2)
-        copies = exchange(
-            lambda side: halo_send.at[step, side], lambda side: extended[step].at[pl.ds(nb + side * nh, nh)],
-            lambda side: halo_ssem.at[step, side], lambda side: halo_rsem.at[step, side],
+        lax.fori_loop(0, nh, gather_block, 0, unroll=4)
+        return to_partner(
+            halo_send.at[step], extended[step].at[pl.ds(nb + (1 - served) * nh, nh)], halo_ssem.at[step], halo_rsem.at[step]
         )
-        for copy in copies:
-            copy.start()
-        return copies
 
     def send_returns(step):
-        col_products(lambda b: own[b])
-        for side in range(2):
-            for c in range(nh):
-                ret_send[step, side, c] = col_sums[table[COL_END, nb + side * nh + c]].astype(RETURN_TYPE)
-        copies = exchange(
-            lambda side: ret_send.at[step, side], lambda side: ret_recv.at[step, side],
-            lambda side: ret_ssem.at[step, side], lambda side: ret_rsem.at[step, side],
+        products(lambda b: own[b], tiles, col_sums, BY_COL)
+        for c in range(nh):
+            ret_send[step, c] = col_sums[table[COL_END, nb + served * nh + c]].astype(RETURN_TYPE)
+        return to_partner(ret_send.at[step], ret_recv.at[step], ret_ssem.at[step], ret_rsem.at[step])
+
+    def part_copy(step, piece):
+        where = pl.ds(piece * (nb // PIECES), nb // PIECES)
+        return pltpu.make_async_remote_copy(
+            src_ref=part_send.at[step, where], dst_ref=part_recv.at[step, where],
+            send_sem=part_ssem.at[step, piece], recv_sem=part_rsem.at[step, piece],
+            device_id={"probe": sibling}, device_id_type=MESH,
         )
-        for copy in copies:
-            copy.start()
-        return copies
-
-    def combine(step, source, target):
+
+    def send_parts(step):
         def body(block, carry):
-            total = row_sums[table[ROW_END, block]] + col_sums[table[COL_END, block]]
-            for side in range(2):
-                where = jnp.broadcast_to(inverse[pl.ds(side * nb + block, 1), :], (8, LANES))
-                total = total + found_of(lambda s: ret_recv[step, side, s], where, nh, f32)
-            root = root_of(block)
-            put_block(target, block, -(root * (root * block_of(source, block) + total)))
+            total = row_sums[table[ROW_END, block]] + mine * col_sums[table[COL_END, block]]
+            where = jnp.broadcast_to(inverse[pl.ds(served * nb + block, 1), :], (8, LANES))
+            part_send[step, block] = total + found_of(lambda s: ret_recv[step, s], where, nh)
             return carry
 
-        lax.fori_loop(0, nb, body, 0, unroll=4)
-
-    start_at, image_at = 0, STEPS + 4
+        size = nb // PIECES
+        for piece in range(PIECES):
+            lax.fori_loop(piece * size, (piece + 1) * size, body, 0, unroll=8)
+            part_copy(step, piece).start()
+
+    def image_of(step, source, block):
+        root = root_of(block)
+        return -(root * (root * block_of(source, block) + (part_send[step, block] + part_recv[step, block])))
+
+    start_at = 0
 
     def q_at(j):
         return j
@@ -398,53 +432,54 @@
     def u_at(j):
         return STEPS + j
 
+    def close(step, gram, coupling):
+        shift = gram[8:]
+        rest = minus(gram[:8], outer(shift))
+        if coupling is not None:
+            rest = minus(rest, outer(coupling))
+        factor, inv_cols, next_coupling = factorise(rest)
+        put_matrix(step - 1, [column + jnp.where(sub == q, 1.0, 0.0) for q, column in enumerate(shift)])
+        put_matrix(STEPS + step - 1, factor)
+        less = [[-column for column in product(inv_cols, shift)]]
+        if coupling is not None:
+            less.append([-column for column in product(inv_cols, coupling)])
+        return inv_cols, less, next_coupling
+
+    def scale_start(block, carry):
+        scale_block(0, block, block_of(start_at, block))
+        return carry
+
+    lax.fori_loop(0, nb, scale_start, 0, unroll=4)
     coupling = None
     for step in range(STEPS):
-        source = start_at if step == 0 else u_at(step)
-
-        if step == 0:
-            def body(block, carry):
-                scale_block(0, block, block_of(start_at, block))
-                return carry
-
-            lax.fori_loop(0, nb, body, 0, unroll=4)
-        halos = send_halo(step)
-        returns = send_returns(step)
+        source = u_at(step) if step else start_at
+        halo = send_halo(step)
         if step:
-            mix(q_terms, q_at(step))
-            gram_begin(step, grams([(u_at(step), u_at(step)), (u_at(step), q_at(step))]))
-        for copy in halos:
-            copy.wait()
-        row_products(lambda b: extended[step][b])
-
-        if step == 0:
-            factor, inv_cols, next_coupling = factorise(gram_end(0, 8))
-            q_terms = [(inv_cols, start_at)]
-            u_terms = [(inv_cols, image_at)]
+            gram_begin(step, grams([(source, source), (source, q_at(step))]))
+        returned = send_returns(step)
+        halo.wait()
+        products(lambda b: extended[step][b], turned, row_sums, BY_ROW)
+        returned.wait()
+        send_parts(step)
+        gram = gram_end(step, 16 if step else 8)
+        if step:
+            inv_cols, less, coupling = close(step, gram, coupling)
         else:
-            gram = gram_end(step, 16)
-            shift = gram[8:]
-            rest = minus(gram[:8], outer(shift))
-            if step > 1:
-                rest = minus(rest, outer(coupling))
-            factor, inv_cols, next_coupling = factorise(rest)
-            put_matrix(step - 1, [column + jnp.where(sub == q, 1.0, 0.0) for q, column in enumerate(shift)])
-            put_matrix(STEPS + step - 1, factor)
-            less = [-column for column in product(inv_cols, shift)]
-            q_terms = [(inv_cols, u_at(step)), (less, q_at(step))]
-            u_terms = [(inv_cols, image_at), (less, u_at(step))]
-            if step > 1:
-                less = [-column for column in product(inv_cols, coupling)]
-                q_terms.append((less, q_at(step - 1)))
-                u_terms.append((less, u_at(step - 1)))
-        coupling = next_coupling
-
-        for copy in returns:
-            copy.wait()
-        combine(step, source, image_at)
+            _, inv_cols, _ = factorise(gram)
+            less = []
+        q_terms = [(inv_cols, source)] + [(columns, q_at(step - i)) for i, columns in enumerate(less)]
+        mix(q_terms, q_at(step + 1))
+        for piece in range(PIECES):
+            part_copy(step, piece).wait()
+        u_terms = [(columns, u_at(step - i)) for i, columns in enumerate(less)]
 
         def next_image(block, carry):
-            value = mixed(u_terms, block)
+            image = image_of(step, source, block)
+            value = inv_cols[0] * spread(image, 0)
+            for q in range(1, 8):
+                value = value + inv_cols[q] * spread(image, q)
+            if u_terms:
+                value = value + mixed(u_terms, block)
             put_block(u_at(step + 1), block, value)
             if step + 1 < STEPS:
                 scale_block(step + 1, block, value)
@@ -452,25 +487,20 @@
 
         lax.fori_loop(0, nb, next_image, 0, unroll=4)
 
-    mix(q_terms, q_at(STEPS))
     gram_begin(STEPS, grams([(u_at(STEPS), u_at(STEPS)), (u_at(STEPS), q_at(STEPS))]))
     gram = gram_end(STEPS, 16)
-    shift = gram[8:]
-    rest = minus(minus(gram[:8], outer(shift)), outer(coupling))
-    factor, inv_cols, _ = factorise(rest)
-    put_matrix(STEPS - 1, [column + jnp.where(sub == q, 1.0, 0.0) for q, column in enumerate(shift)])
-    put_matrix(2 * STEPS - 1, factor)
-    q_terms = [
-        (inv_cols, u_at(STEPS)),
-        ([-column for column in product(inv_cols, shift)], q_at(STEPS)),
-        ([-column for column in product(inv_cols, coupling)], q_at(STEPS - 1)),
-    ]
+    inv_cols, less, _ = close(STEPS, gram, coupling)
+    q_terms = [(inv_cols, u_at(STEPS))] + [(columns, q_at(STEPS - i)) for i, columns in enumerate(less)]
     mix(q_terms, start_at)
     for p in range(probes_dev):
         for b in range(nb):
             basis_ref[p : p + 1, b * LANES : (b + 1) * LANES] = vec[
                 start_at, pl.ds(b * 8 + my_probe * probes_dev + p, 1), :
             ]
+
+
+def in_hbm(value):
+    return pltpu.with_memory_space_constraint(value, pltpu.HBM)
 
 
 def local(start_block, blocks, block_rows, block_cols, counts, boundary):
@@ -481,7 +511,6 @@
     nh = nb // 2
     f32, bf16 = jnp.float32, jnp.bfloat16
     vmem = pl.BlockSpec(memory_space=pltpu.VMEM)
-    smem = pl.BlockSpec(memory_space=pltpu.SMEM)
     dma = pltpu.SemaphoreType.DMA
     height = 8 * PLANES
     basis, coef = pl.pallas_call(
@@ -490,12 +519,18 @@
             jax.ShapeDtypeStruct((probes_dev, rows_dev), f32),
             jax.ShapeDtypeStruct((2 * STEPS, 8, LANES), f32),
         ),
-        in_specs=[vmem, pl.BlockSpec(memory_space=pltpu.HBM), vmem, vmem, smem, vmem],
+        in_specs=[pl.BlockSpec(memory_space=pltpu.HBM)] * 6,
         out_specs=(vmem, vmem),
         scratch_shapes=[
+            pltpu.VMEM(start_block.shape, f32),
             pltpu.VMEM(blocks.shape, bf16),
+            pltpu.VMEM(blocks.shape, bf16),
+            pltpu.VMEM((1, slots), jnp.int32),
+            pltpu.VMEM((1, slots), jnp.int32),
+            pltpu.SMEM(counts.shape, jnp.int32),
+            pltpu.VMEM(boundary.shape, jnp.int32),
             pltpu.VMEM((n_probe, probes_dev, rows_dev), f32),
-            pltpu.VMEM((2 * STEPS + 2, nb * 8, LANES), f32),
+            pltpu.VMEM((2 * STEPS + 1, nb * 8, LANES), f32),
             pltpu.VMEM((nb * 8, LANES), f32),
             pltpu.VMEM((nb, LANES), f32),
             pltpu.VMEM((2 * nb, LANES), jnp.int32),
@@ -503,34 +538,39 @@
             pltpu.SMEM((8, LANES), jnp.int32),
             pltpu.VMEM((nb, height, LANES), bf16),
             *[pltpu.VMEM((2 * nb, height, LANES), bf16)] * STEPS,
-            pltpu.VMEM((STEPS, 2, nh, height, LANES), bf16),
-            pltpu.VMEM((STEPS, 2, nh, 8, LANES), RETURN_TYPE),
-            pltpu.VMEM((STEPS, 2, nh, 8, LANES), RETURN_TYPE),
+            pltpu.VMEM((STEPS, nh, height, LANES), bf16),
+            pltpu.VMEM((STEPS, nh, 8, LANES), RETURN_TYPE),
+            pltpu.VMEM((STEPS, nh, 8, LANES), RETURN_TYPE),
             pltpu.VMEM((2, nh, LANES), f32),
             pltpu.VMEM((2, nh, LANES), f32),
+            pltpu.VMEM((STEPS, nb, 8, LANES), f32),
+            pltpu.VMEM((STEPS, nb, 8, LANES), f32),
             pltpu.VMEM((slots + 1, 8, LANES), f32),
             pltpu.VMEM((slots + 1, 8, LANES), f32),
             pltpu.VMEM((STEPS + 1, 8, LANES), f32),
             pltpu.VMEM((STEPS + 1, n_rows, 8, LANES), f32),
-            dma,
+            dma((6,)),
             dma,
             dma((n_probe,)),
             dma((n_probe,)),
-            dma((STEPS, 2)),
-            dma((STEPS, 2)),
-            dma((STEPS, 2)),
-            dma((STEPS, 2)),
+            dma((STEPS,)),
+            dma((STEPS,)),
+            dma((STEPS,)),
+            dma((STEPS,)),
+            dma((STEPS, PIECES)),
+            dma((STEPS, PIECES)),
             dma((2,)),
             dma((2,)),
             dma((STEPS + 1, n_rows)),
             dma((STEPS + 1, n_rows)),
         ],
         compiler_params=pltpu.CompilerParams(
-            collective_id=0, has_side_effects=True, vmem_limit_bytes=48 * 1024 * 1024
+            collective_id=0, has_side_effects=True, vmem_limit_bytes=VMEM_BYTES
         ),
         name="lanczos",
     )(
-        start_block, blocks, block_rows.reshape(1, slots), block_cols.reshape(1, slots), counts, boundary,
+        in_hbm(start_block), in_hbm(blocks), in_hbm(block_rows.reshape(1, slots)),
+        in_hbm(block_cols.reshape(1, slots)), counts, in_hbm(boundary),
     )
     return basis, coef[:STEPS, :, :8], coef[STEPS:, :, :8]
 

time: 65.3 us -> 44.1 us (0.68)
  Pallas kernels: 57.5 us -> 41.4 us
  local copies, waits for them, and re-layouts: 6.19 us -> 1.22 us
    pallas_call x1, Pallas kernels: 57.5 us -> 41.4 us  [local(): pl.pallas_call(functools.partial(kernel, n_rows, n_probe, rows_dev * n_ro...]
    unnamed x11 -> x1, local copies, waits for them, and re-layouts: 5.58 us -> 0.61 us
where the time goes in v2:
time: 44.1 us; the launch traced here: 43.9 us
  Pallas kernels  41.4 us (94%)
  between operations  1.29 us (3%)
  local copies, waits for them, and re-layouts  1.22 us (3%)
    pallas_call x1, Pallas kernels, local(): pl.pallas_call(functools.partial(kernel, n_rows, n_probe, rows_dev * n_ro...  41.4 us

profile of v2, /device:TPU:0, one launch (start us, length us, event | category | flops | bytes accessed | tf_op | source)
XLA Modules:
  0.0 43.9 jit_solution(18163286641538607766)
XLA Ops:
  1.3 41.4 %lanczos.1 = (f32[2,4096]{1,0:T(2,128)S(1)}, f32[6,8,128]{2,1,0:T(8,128)S(1)}) custom-call(f32[2,4096]{1,0:T(2,128)} %start_hbm.1, bf16[128,128,128]{2,1,0:T(8,128)(2,1)} %tiles_hbm.1, s32[1,128]{1,0:T(1,128)} %bitcast.2, s32[1,128]{1,0:T(1,128)} %bitcast.3, s32[1]{0:T(128)S(6)} %copy.10.counts_hbm, s32[2,2048]{1,0:T(2,128)} %bound_hbm.1), custom_call_target="tpu_custom_call" | custom-call | tf_op jit(solution)/shard_map/lanczos/pallas_call | solution.py:516
  42.7 0.6 %fusion = (f32[3,8,8]{2,1,0:T(8,128)}, f32[3,8,8]{2,1,0:T(8,128)}) fusion(f32[6,8,128]{2,1,0:T(8,128)S(1)} %get-tuple-element.6), kind=kLoop, calls=%fused_computation | loop fusion | bytes 3072 | tf_op jit(solution)/shard_map/slice | solution.py:575
  43.3 0.6 %copy.11 = f32[2,4096]{1,0:T(2,128)} copy(f32[2,4096]{1,0:T(2,128)S(1)} %get-tuple-element.12) | data formatting | bytes 65536

commit v3 on v2

--- a/solution.py
+++ b/solution.py
@@ -9,10 +9,8 @@
 
 STEPS = 3
 LANES = 128
-PLANES = 2
 PIECES = 4
 VMEM_BYTES = 48 * 1024 * 1024
-RETURN_TYPE = jnp.float32
 MESH = pl.DeviceIdType.MESH
 BY_COL, COL_OTHER, COL_END, COL_KEEP, BY_ROW, ROW_OTHER, ROW_END, ROW_KEEP = range(8)
 
@@ -21,9 +19,10 @@
     n_rows, n_probe, node_total,
     start_hbm, tiles_hbm, rows_hbm, cols_hbm, counts_hbm, bound_hbm,
     basis_ref, coef_ref,
-    start_ref, tiles, turned, rows_ref, cols_ref, counts_ref, bound_ref, gathered, vec, scaled, inv_root, inverse, table_v, table,
-    own, extended_0, extended_1, extended_2, halo_send, ret_send, ret_recv, deg_send, deg_recv, part_send, part_recv, row_sums, col_sums, gram_send, gram_recv,
-    load_sem, table_sem, start_send, start_recv, halo_ssem, halo_rsem, ret_ssem, ret_rsem, part_ssem, part_rsem, deg_ssem, deg_rsem,
+    start_ref, tiles, turned, rows_ref, cols_ref, counts_ref, bound_ref, gathered, vec, spare, scaled, inv_root, inverse, table_v, table,
+    boundary_of, own, extended, start_halo_send, start_halo_recv, root_halo_send, root_halo_recv, halo_send, halo_recv,
+    first_send, first_recv, ret_send, ret_recv, returned, deg_send, deg_recv, part_send, part_recv, row_sums, col_sums, gram_send, gram_recv,
+    load_sem, table_sem, start_send, start_recv, root_ssem, root_rsem, halo_ssem, halo_rsem, ret_ssem, ret_rsem, part_ssem, part_rsem, deg_ssem, deg_rsem,
     gram_ssem, gram_rsem,
 ):
     me = lax.axis_index("rows")
@@ -39,17 +38,12 @@
     served = 1 - lax.rem(me + half, 2)
     partner = lax.rem(me + 2 * served - 1 + n_rows, n_rows)
     f32, bf16 = jnp.float32, jnp.bfloat16
-    extended = (extended_0, extended_1, extended_2)
-
-    loads = [
-        pltpu.make_async_copy(source, target, load_sem.at[i])
-        for i, (source, target) in enumerate(
-            (
-                (rows_hbm, rows_ref), (cols_hbm, cols_ref), (counts_hbm, counts_ref), (start_hbm, start_ref),
-                (bound_hbm, bound_ref), (tiles_hbm, tiles),
-            )
-        )
-    ]
+
+    moves = (
+        (rows_hbm, rows_ref), (cols_hbm, cols_ref), (counts_hbm, counts_ref), (start_hbm, start_ref),
+        (bound_hbm, bound_ref), (tiles_hbm, tiles),
+    )
+    loads = [pltpu.make_async_copy(source, target, load_sem.at[i]) for i, (source, target) in enumerate(moves)]
     for load in loads:
         load.start()
 
@@ -60,7 +54,8 @@
 
     def greet(off, carry):
         peer = lax.rem(me + off, n_rows)
-        pl.semaphore_signal(barrier, inc=1, device_id={"rows": peer}, device_id_type=MESH)
+        for probe in (my_probe, sibling):
+            pl.semaphore_signal(barrier, inc=1, device_id={"rows": peer, "probe": probe}, device_id_type=MESH)
         return carry
 
     lax.fori_loop(1, n_rows, greet, 0)
@@ -106,15 +101,24 @@
     table_copy = pltpu.make_async_copy(table_v, table, table_sem)
     table_copy.start()
 
-    pl.semaphore_wait(barrier, n_probe - 1 + n_rows - 1)
+    pl.semaphore_wait(barrier, n_probe - 1 + 2 * (n_rows - 1))
+
+    def arrived(ref, send_sem, recv_sem):
+        return pltpu.make_async_remote_copy(
+            src_ref=ref, dst_ref=ref, send_sem=send_sem, recv_sem=recv_sem,
+            device_id={"probe": sibling}, device_id_type=MESH,
+        )
+
+    def wait_for(ref, send_sem, recv_sem):
+        arrived(ref, send_sem, recv_sem).wait()
 
     def start_copy(off):
         peer = lax.rem(my_probe + off, n_probe)
         return pltpu.make_async_remote_copy(
             src_ref=start_ref,
             dst_ref=gathered.at[my_probe],
-            send_sem=start_send.at[off],
-            recv_sem=start_recv.at[off],
+            send_sem=start_send,
+            recv_sem=start_recv,
             device_id={"probe": peer},
             device_id_type=MESH,
         )
@@ -124,6 +128,28 @@
         start_copy(off).start()
     gathered[my_probe] = start_ref[...]
     table_copy.wait()
+    loads[4].wait()
+    for c in range(nh):
+        where = slice(c * LANES, (c + 1) * LANES)
+        boundary_of[c : c + 1, :] = jnp.where(served == 1, bound_ref[1:2, where], bound_ref[0:1, where])
+    sub_l = lax.broadcasted_iota(jnp.int32, (LANES, LANES), 0)
+    sub_b = lax.broadcasted_iota(jnp.int32, (nb, LANES), 0)
+    lane_b = lax.broadcasted_iota(jnp.int32, (nb, LANES), 1)
+    for side in range(2):
+        total = jnp.zeros((2 * nb, LANES), f32)
+        for c in range(nh):
+            where = bound_ref[side : side + 1, c * LANES : (c + 1) * LANES]
+            in_block = sub_b == jnp.broadcast_to(jnp.right_shift(where, 7), (nb, LANES))
+            at_lane = sub_l == jnp.broadcast_to(jnp.bitwise_and(where, LANES - 1), (LANES, LANES))
+            h = lane_b + c * LANES
+            high = jnp.where(in_block, (jnp.right_shift(h, 6) + 1).astype(f32), 0.0)
+            low = jnp.where(in_block, jnp.bitwise_and(h, 63).astype(f32), 0.0)
+            total = total + lax.dot_general(
+                jnp.concatenate([high, low], axis=0).astype(bf16), jnp.where(at_lane, 1.0, 0.0).astype(bf16),
+                (((1,), (1,)), ((), ())), preferred_element_type=f32,
+            )
+        inverse[pl.ds(side * nb, nb), :] = ((total[:nb] - 1.0) * 64.0 + total[nb:]).astype(jnp.int32)
+
 
     def row_of(k, block, probe):
         return jnp.broadcast_to(vec[k, pl.ds(block * 8 + probe, 1), :], (8, LANES))
@@ -137,14 +163,14 @@
     def root_of(block):
         return jnp.broadcast_to(inv_root[pl.ds(block, 1), :], (8, LANES))
 
-    def gram_copy(index, off):
+    def gram_copy(index, off, probe):
         peer = lax.rem(me + off, n_rows)
         return pltpu.make_async_remote_copy(
             src_ref=gram_send.at[index],
             dst_ref=gram_recv.at[index, me],
-            send_sem=gram_ssem.at[index, off],
-            recv_sem=gram_rsem.at[index, off],
-            device_id={"rows": peer},
+            send_sem=gram_ssem.at[index],
+            recv_sem=gram_rsem.at[index],
+            device_id={"rows": peer, "probe": probe},
             device_id_type=MESH,
         )
 
@@ -156,17 +182,23 @@
         gram_recv[index, me] = gram
 
         def send(off, carry):
-            gram_copy(index, off).start()
+            for probe in (sibling, my_probe):
+                gram_copy(index, off, probe).start()
             return carry
 
-        lax.fori_loop(1, n_rows, send, 0)
+        @pl.when(half == 1)
+        def _():
+            lax.fori_loop(1, n_rows, send, 0)
 
     def gram_end(index, count):
-        def wait(off, carry):
-            gram_copy(index, off).wait()
-            return carry
-
-        lax.fori_loop(1, n_rows, wait, 0)
+        others = gram_recv.at[index, pl.ds(0, n_rows - 1)]
+        arrived(others, gram_ssem.at[index], gram_rsem.at[index]).wait_recv()
+
+        @pl.when(half == 1)
+        def _():
+            for _ in range(2):
+                arrived(others, gram_ssem.at[index], gram_rsem.at[index]).wait_send()
+
         gram = jnp.sum(gram_recv[index], axis=0) * (1.0 / node_total)
         return [jnp.broadcast_to(gram[:, q : q + 1], (8, LANES)) for q in range(count)]
 
@@ -247,7 +279,7 @@
     def folded(value):
         return value if value.shape[0] == 8 else value[:8] + value[8:]
 
-    def products(lhs_of, source, sums, first):
+    def products(lhs_of, source, sums, first, beside=()):
         by, other, keep = first + BY_COL, first + COL_OTHER, first + COL_KEEP
         acc = zero
         for m in range(0, slots, 2):
@@ -264,6 +296,8 @@
                 part = y[i * height : (i + 1) * height, i * LANES : (i + 1) * LANES]
                 acc = acc * table[keep, k].astype(f32) + folded(part)
                 sums[k] = acc
+            for task in range(m * len(beside) // slots, (m + 2) * len(beside) // slots):
+                beside[task]()
 
     row_sums[slots] = zero
     col_sums[slots] = zero
@@ -281,7 +315,84 @@
             for side in range(2)
         ]
 
-    loads[4].wait()
+    def found_of(source_of, where, count):
+        spot = jnp.bitwise_and(where, LANES - 1)
+        block = jnp.right_shift(where, 7)
+        found = zero
+        for s in range(count):
+            picked = jnp.take_along_axis(source_of(s).astype(f32), spot, axis=1, mode="promise_in_bounds")
+            found = jnp.where(block == s, picked, found)
+        return found
+
+    mine = (1 - half).astype(f32)
+
+    def planes(value):
+        top = value.astype(bf16)
+        return jnp.concatenate([top, (value - top.astype(f32)).astype(bf16)], axis=0)
+
+    def scale_block(block, value):
+        value = root_of(block) * value
+        scaled[pl.ds(pl.multiple_of(block * 8, 8), 8), :] = value
+        own[block] = planes(value)
+        extended[block] = planes(value * mine)
+
+    for c in range(nh):
+        extended[nb + (1 - served) * nh + c] = jnp.zeros((16, LANES), bf16)
+
+    def to_partner(src_ref, dst_ref, send_sem, recv_sem):
+        copy = pltpu.make_async_remote_copy(
+            src_ref=src_ref, dst_ref=dst_ref, send_sem=send_sem, recv_sem=recv_sem,
+            device_id={"rows": partner}, device_id_type=MESH,
+        )
+        copy.start()
+        return copy
+
+    def boundary_row(c):
+        return jnp.broadcast_to(boundary_of[c : c + 1, :], (8, LANES))
+
+    def send_start_halo():
+        for c in range(nh):
+            start_halo_send[c] = found_of(lambda s: block_of(0, s), boundary_row(c), nb)
+        return to_partner(start_halo_send, start_halo_recv, halo_ssem.at[0], halo_rsem.at[0])
+
+    def send_root_halo():
+        for g in range(nh // 8):
+            where = boundary_of[g * 8 : g * 8 + 8, :]
+            root_halo_send[g * 8 : g * 8 + 8, :] = found_of(
+                lambda s: jnp.broadcast_to(inv_root[s : s + 1, :], (8, LANES)), where, nb
+            )
+        return to_partner(root_halo_send, root_halo_recv, root_ssem, root_rsem)
+
+    def gather_block(step, c):
+        found = found_of(lambda s: scaled[s * 8 : s * 8 + 8, :], boundary_row(c), nb)
+        halo_send[step, c] = found.astype(bf16)
+
+    def send_halo(step):
+        return to_partner(halo_send.at[step], halo_recv.at[step], halo_ssem.at[step], halo_rsem.at[step])
+
+    def take_halo(step):
+        for c in range(nh):
+            if step:
+                pieces = jnp.concatenate([halo_recv[step, c], jnp.zeros((8, LANES), bf16)], axis=0)
+            else:
+                pieces = planes(jnp.broadcast_to(root_halo_recv[c : c + 1, :], (8, LANES)) * start_halo_recv[c])
+            extended[nb + served * nh + c] = pieces
+
+    def send_returns(step):
+        send, recv = (ret_send.at[step], ret_recv.at[step]) if step else (first_send, first_recv)
+        for c in range(nh):
+            send[c] = col_sums[table[COL_END, nb + served * nh + c]].astype(send.dtype)
+        return to_partner(send, recv, ret_ssem.at[step], ret_rsem.at[step])
+
+    def take_returns(step):
+        for c in range(nh):
+            returned[c] = ret_recv[step, c].astype(f32)
+
+    def scatter_block(step, block):
+        where = jnp.broadcast_to(inverse[pl.ds(served * nb + block, 1), :], (8, LANES))
+        source = returned if step else first_recv
+        part_send[step, block] = found_of(lambda s: source[s], where, nh)
+
     loads[5].wait()
     ones = jnp.concatenate([jnp.ones((8, LANES), bf16), jnp.zeros((8, LANES), bf16)], axis=0)
     products(lambda b: ones, tiles, col_sums, BY_COL)
@@ -295,7 +406,6 @@
     for copy in deg_copies:
         copy.start()
 
-
     def turn(t, carry):
         turned[t] = tiles[t].T
         return carry
@@ -303,35 +413,7 @@
     lax.fori_loop(0, slots, turn, 0, unroll=16)
     products(lambda b: ones, turned, row_sums, BY_ROW)
 
-    sub_l = lax.broadcasted_iota(jnp.int32, (LANES, LANES), 0)
-    sub_b = lax.broadcasted_iota(jnp.int32, (nb, LANES), 0)
-    lane_b = lax.broadcasted_iota(jnp.int32, (nb, LANES), 1)
-    for side in range(2):
-        total = jnp.zeros((2 * nb, LANES), f32)
-        for c in range(nh):
-            where = bound_ref[side : side + 1, c * LANES : (c + 1) * LANES]
-            in_block = sub_b == jnp.broadcast_to(jnp.right_shift(where, 7), (nb, LANES))
-            at_lane = sub_l == jnp.broadcast_to(jnp.bitwise_and(where, LANES - 1), (LANES, LANES))
-            h = lane_b + c * LANES
-            high = jnp.where(in_block, (jnp.right_shift(h, 6) + 1).astype(f32), 0.0)
-            low = jnp.where(in_block, jnp.bitwise_and(h, 63).astype(f32), 0.0)
-            total = total + lax.dot_general(
-                jnp.concatenate([high, low], axis=0).astype(bf16), jnp.where(at_lane, 1.0, 0.0).astype(bf16),
-                (((1,), (1,)), ((), ())), preferred_element_type=f32,
-            )
-        inverse[pl.ds(side * nb, nb), :] = ((total[:nb] - 1.0) * 64.0 + total[nb:]).astype(jnp.int32)
-
-    def found_of(source_of, where, count):
-        spot = jnp.bitwise_and(where, LANES - 1)
-        block = jnp.right_shift(where, 7)
-        found = zero
-        for s in range(count):
-            picked = jnp.take_along_axis(source_of(s).astype(f32), spot, axis=1, mode="promise_in_bounds")
-            found = jnp.where(block == s, picked, found)
-        return found
-
-    for off in range(1, n_probe):
-        start_copy(off).wait()
+    wait_for(gathered.at[pl.ds(0, n_probe - 1)], start_send, start_recv)
 
     def take_start(block, carry):
         where = pl.ds(pl.multiple_of(block * LANES, LANES), LANES)
@@ -341,6 +423,7 @@
 
     lax.fori_loop(0, nb, take_start, 0, unroll=8)
     gram_begin(0, grams([(0, 0)]))
+    start_halo = send_start_halo()
     for b in range(nb):
         inv_root[b : b + 1, :] = row_sums[table[ROW_END, b], 0:1, :] + col_sums[table[COL_END, b], 0:1, :]
     for copy in deg_copies:
@@ -355,69 +438,21 @@
         inv_root[g * 8 : g * 8 + 8, :] = 1.0 / jnp.sqrt(degree)
 
 
-    def planes(value):
-        top = value.astype(bf16)
-        if PLANES == 1:
-            return top
-        return jnp.concatenate([top, (value - top.astype(f32)).astype(bf16)], axis=0)
-
-    mine = (1 - half).astype(f32)
-
-    def scale_block(step, block, value):
-        value = root_of(block) * value
-        scaled[pl.ds(pl.multiple_of(block * 8, 8), 8), :] = value
-        own[block] = planes(value)
-        extended[step][block] = planes(value * mine)
-
-    for step in range(STEPS):
-        for c in range(nh):
-            extended[step][nb + (1 - served) * nh + c] = jnp.zeros((8 * PLANES, LANES), bf16)
-
-    def to_partner(src_ref, dst_ref, send_sem, recv_sem):
-        copy = pltpu.make_async_remote_copy(
-            src_ref=src_ref, dst_ref=dst_ref, send_sem=send_sem, recv_sem=recv_sem,
-            device_id={"rows": partner}, device_id_type=MESH,
-        )
-        copy.start()
-        return copy
-
-    def send_halo(step):
-        def gather_block(c, carry):
-            where = pl.ds(pl.multiple_of(c * LANES, LANES), LANES)
-            piece = jnp.where(served == 1, bound_ref[1:2, where], bound_ref[0:1, where])
-            found = found_of(lambda s: scaled[s * 8 : s * 8 + 8, :], jnp.broadcast_to(piece, (8, LANES)), nb)
-            halo_send[step, c] = planes(found)
-            return carry
-
-        lax.fori_loop(0, nh, gather_block, 0, unroll=4)
-        return to_partner(
-            halo_send.at[step], extended[step].at[pl.ds(nb + (1 - served) * nh, nh)], halo_ssem.at[step], halo_rsem.at[step]
-        )
-
-    def send_returns(step):
-        products(lambda b: own[b], tiles, col_sums, BY_COL)
-        for c in range(nh):
-            ret_send[step, c] = col_sums[table[COL_END, nb + served * nh + c]].astype(RETURN_TYPE)
-        return to_partner(ret_send.at[step], ret_recv.at[step], ret_ssem.at[step], ret_rsem.at[step])
-
     def part_copy(step, piece):
         where = pl.ds(piece * (nb // PIECES), nb // PIECES)
         return pltpu.make_async_remote_copy(
             src_ref=part_send.at[step, where], dst_ref=part_recv.at[step, where],
-            send_sem=part_ssem.at[step, piece], recv_sem=part_rsem.at[step, piece],
+            send_sem=part_ssem.at[step], recv_sem=part_rsem.at[step],
             device_id={"probe": sibling}, device_id_type=MESH,
         )
 
     def send_parts(step):
-        def body(block, carry):
-            total = row_sums[table[ROW_END, block]] + mine * col_sums[table[COL_END, block]]
-            where = jnp.broadcast_to(inverse[pl.ds(served * nb + block, 1), :], (8, LANES))
-            part_send[step, block] = total + found_of(lambda s: ret_recv[step, s], where, nh)
-            return carry
-
         size = nb // PIECES
         for piece in range(PIECES):
-            lax.fori_loop(piece * size, (piece + 1) * size, body, 0, unroll=8)
+            for block in range(piece * size, (piece + 1) * size):
+                part_send[step, block] = (
+                    part_send[step, block] + row_sums[table[ROW_END, block]] + mine * col_sums[table[COL_END, block]]
+                )
             part_copy(step, piece).start()
 
     def image_of(step, source, block):
@@ -446,20 +481,41 @@
         return inv_cols, less, next_coupling
 
     def scale_start(block, carry):
-        scale_block(0, block, block_of(start_at, block))
+        scale_block(block, block_of(start_at, block))
         return carry
 
+    root_halo = send_root_halo()
     lax.fori_loop(0, nb, scale_start, 0, unroll=4)
     coupling = None
     for step in range(STEPS):
         source = u_at(step) if step else start_at
-        halo = send_halo(step)
+        accs = [zero] * 16
+
+        def gram_block(block):
+            image = block_of(source, block)
+            for q in range(8):
+                accs[q] = accs[q] + image * row_of(source, block, q)
+                accs[8 + q] = accs[8 + q] + image * row_of(q_at(step), block, q)
+
+        beside = []
         if step:
-            gram_begin(step, grams([(source, source), (source, q_at(step))]))
-        returned = send_returns(step)
+            for c in range(nh):
+                beside.append(functools.partial(gather_block, step, c))
+                beside += [functools.partial(gram_block, 2 * c + i) for i in range(2)]
+        products(lambda b: own[b], tiles, col_sums, BY_COL, beside)
+        halo = send_halo(step) if step else start_halo
+        returns = send_returns(step)
+        if step:
+            gram_begin(step, accs)
         halo.wait()
-        products(lambda b: extended[step][b], turned, row_sums, BY_ROW)
-        returned.wait()
+        if step == 0:
+            root_halo.wait()
+        take_halo(step)
+        returns.wait()
+        if step:
+            take_returns(step)
+        scatters = [functools.partial(scatter_block, step, block) for block in range(nb)]
+        products(lambda b: extended[b], turned, row_sums, BY_ROW, scatters)
         send_parts(step)
         gram = gram_end(step, 16 if step else 8)
         if step:
@@ -467,11 +523,12 @@
         else:
             _, inv_cols, _ = factorise(gram)
             less = []
+        u_terms = [(columns, u_at(step - i)) for i, columns in enumerate(less)]
+        if u_terms:
+            mix(u_terms, u_at(step + 1))
         q_terms = [(inv_cols, source)] + [(columns, q_at(step - i)) for i, columns in enumerate(less)]
         mix(q_terms, q_at(step + 1))
-        for piece in range(PIECES):
-            part_copy(step, piece).wait()
-        u_terms = [(columns, u_at(step - i)) for i, columns in enumerate(less)]
+        wait_for(part_recv.at[step], part_ssem.at[step], part_rsem.at[step])
 
         def next_image(block, carry):
             image = image_of(step, source, block)
@@ -479,10 +536,10 @@
             for q in range(1, 8):
                 value = value + inv_cols[q] * spread(image, q)
             if u_terms:
-                value = value + mixed(u_terms, block)
+                value = value + block_of(u_at(step + 1), block)
             put_block(u_at(step + 1), block, value)
             if step + 1 < STEPS:
-                scale_block(step + 1, block, value)
+                scale_block(block, value)
             return carry
 
         lax.fori_loop(0, nb, next_image, 0, unroll=4)
@@ -490,13 +547,17 @@
     gram_begin(STEPS, grams([(u_at(STEPS), u_at(STEPS)), (u_at(STEPS), q_at(STEPS))]))
     gram = gram_end(STEPS, 16)
     inv_cols, less, _ = close(STEPS, gram, coupling)
-    q_terms = [(inv_cols, u_at(STEPS))] + [(columns, q_at(STEPS - i)) for i, columns in enumerate(less)]
-    mix(q_terms, start_at)
+    terms = [(inv_cols, u_at(STEPS))] + [(columns, q_at(STEPS - i)) for i, columns in enumerate(less)]
+    for i, (columns, _) in enumerate(terms):
+        for q in range(8):
+            spare[i * 64 + q * 8 : i * 64 + q * 8 + 8, :] = columns[q]
     for p in range(probes_dev):
-        for b in range(nb):
-            basis_ref[p : p + 1, b * LANES : (b + 1) * LANES] = vec[
-                start_at, pl.ds(b * 8 + my_probe * probes_dev + p, 1), :
-            ]
+        total = jnp.zeros((nb, LANES), f32)
+        for i, (_, k) in enumerate(terms):
+            for q in range(8):
+                weight = spare[pl.ds(i * 64 + q * 8 + my_probe * probes_dev + p, 1), :]
+                total = total + jnp.broadcast_to(weight, (nb, LANES)) * vec[k, pl.ds(q, nb, stride=8), :]
+        basis_ref[p] = total
 
 
 def in_hbm(value):
@@ -512,11 +573,10 @@
     f32, bf16 = jnp.float32, jnp.bfloat16
     vmem = pl.BlockSpec(memory_space=pltpu.VMEM)
     dma = pltpu.SemaphoreType.DMA
-    height = 8 * PLANES
     basis, coef = pl.pallas_call(
         functools.partial(kernel, n_rows, n_probe, rows_dev * n_rows),
         out_shape=(
-            jax.ShapeDtypeStruct((probes_dev, rows_dev), f32),
+            jax.ShapeDtypeStruct((probes_dev, nb, LANES), f32),
             jax.ShapeDtypeStruct((2 * STEPS, 8, LANES), f32),
         ),
         in_specs=[pl.BlockSpec(memory_space=pltpu.HBM)] * 6,
@@ -531,16 +591,26 @@
             pltpu.VMEM(boundary.shape, jnp.int32),
             pltpu.VMEM((n_probe, probes_dev, rows_dev), f32),
             pltpu.VMEM((2 * STEPS + 1, nb * 8, LANES), f32),
+            pltpu.VMEM((3 * 64, LANES), f32),
             pltpu.VMEM((nb * 8, LANES), f32),
             pltpu.VMEM((nb, LANES), f32),
             pltpu.VMEM((2 * nb, LANES), jnp.int32),
             pltpu.VMEM((8, LANES), jnp.int32),
             pltpu.SMEM((8, LANES), jnp.int32),
-            pltpu.VMEM((nb, height, LANES), bf16),
-            *[pltpu.VMEM((2 * nb, height, LANES), bf16)] * STEPS,
-            pltpu.VMEM((STEPS, nh, height, LANES), bf16),
-            pltpu.VMEM((STEPS, nh, 8, LANES), RETURN_TYPE),
-            pltpu.VMEM((STEPS, nh, 8, LANES), RETURN_TYPE),
+            pltpu.VMEM((nh, LANES), jnp.int32),
+            pltpu.VMEM((nb, 16, LANES), bf16),
+            pltpu.VMEM((2 * nb, 16, LANES), bf16),
+            pltpu.VMEM((nh, 8, LANES), f32),
+            pltpu.VMEM((nh, 8, LANES), f32),
+            pltpu.VMEM((nh, LANES), f32),
+            pltpu.VMEM((nh, LANES), f32),
+            pltpu.VMEM((STEPS, nh, 8, LANES), bf16),
+            pltpu.VMEM((STEPS, nh, 8, LANES), bf16),
+            pltpu.VMEM((nh, 8, LANES), f32),
+            pltpu.VMEM((nh, 8, LANES), f32),
+            pltpu.VMEM((STEPS, nh, 8, LANES), bf16),
+            pltpu.VMEM((STEPS, nh, 8, LANES), bf16),
+            pltpu.VMEM((nh, 8, LANES), f32),
             pltpu.VMEM((2, nh, LANES), f32),
             pltpu.VMEM((2, nh, LANES), f32),
             pltpu.VMEM((STEPS, nb, 8, LANES), f32),
@@ -551,18 +621,20 @@
             pltpu.VMEM((STEPS + 1, n_rows, 8, LANES), f32),
             dma((6,)),
             dma,
-            dma((n_probe,)),
-            dma((n_probe,)),
+            dma,
+            dma,
+            dma,
+            dma,
             dma((STEPS,)),
             dma((STEPS,)),
             dma((STEPS,)),
             dma((STEPS,)),
-            dma((STEPS, PIECES)),
-            dma((STEPS, PIECES)),
+            dma((STEPS,)),
+            dma((STEPS,)),
             dma((2,)),
             dma((2,)),
-            dma((STEPS + 1, n_rows)),
-            dma((STEPS + 1, n_rows)),
+            dma((STEPS + 1,)),
+            dma((STEPS + 1,)),
         ],
         compiler_params=pltpu.CompilerParams(
             collective_id=0, has_side_effects=True, vmem_limit_bytes=VMEM_BYTES
@@ -572,7 +644,7 @@
         in_hbm(start_block), in_hbm(blocks), in_hbm(block_rows.reshape(1, slots)),
         in_hbm(block_cols.reshape(1, slots)), counts, in_hbm(boundary),
     )
-    return basis, coef[:STEPS, :, :8], coef[STEPS:, :, :8]
+    return basis.reshape(probes_dev, rows_dev), coef[:STEPS, :, :8], coef[STEPS:, :, :8]
 
 
 def solution(mesh):

time: 44.1 us -> 38.8 us (0.88)
  Pallas kernels: 41.4 us -> 36.1 us
    pallas_call x1, Pallas kernels: 41.4 us -> 36.1 us  [local(): pl.pallas_call(functools.partial(kernel, n_rows, n_probe, rows_dev * n_ro...]
where the time goes in v3:
time: 38.8 us; the launch traced here: 38.6 us
  Pallas kernels  36.1 us (93%)
  between operations  1.29 us (3%)
  local copies, waits for them, and re-layouts  1.25 us (3%)
    pallas_call x1, Pallas kernels, local(): pl.pallas_call(functools.partial(kernel, n_rows, n_probe, rows_dev * n_ro...  36.1 us

profile of v3, /device:TPU:0, one launch (start us, length us, event | category | flops | bytes accessed | tf_op | source)
XLA Modules:
  0.0 38.6 jit_solution(1981503939968802633)
XLA Ops:
  1.3 36.1 %lanczos.1 = (f32[2,32,128]{2,1,0:T(8,128)S(1)}, f32[6,8,128]{2,1,0:T(8,128)S(1)}) custom-call(f32[2,4096]{1,0:T(2,128)} %start_hbm.1, bf16[128,128,128]{2,1,0:T(8,128)(2,1)} %tiles_hbm.1, s32[1,128]{1,0:T(1,128)} %bitcast.8, s32[1,128]{1,0:T(1,128)} %bitcast.9, s32[1]{0:T(128)S(6)} %copy.12.counts_hbm, s32[2,2048]{1,0:T(2,128)} %bound_hbm.1), custom_call_target="tpu_custom_call" | custom-call | tf_op jit(solution)/shard_map/lanczos/pallas_call | solution.py:576
  37.4 0.6 %copy.11 = f32[1,2,32,128]{3,1,2,0:T(2,128)} copy(f32[1,2,32,128]{3,2,1,0:T(8,128)S(1)} %bitcast.6) | data formatting | bytes 65536
  38.0 0.6 %fusion = (f32[3,8,8]{2,1,0:T(8,128)}, f32[3,8,8]{2,1,0:T(8,128)}) fusion(f32[6,8,128]{2,1,0:T(8,128)S(1)} %get-tuple-element.6), kind=kLoop, calls=%fused_computation.1 | loop fusion | bytes 3072 | tf_op jit(solution)/shard_map/slice | solution.py:647

commit v4 on v3

--- a/solution.py
+++ b/solution.py
@@ -188,7 +188,7 @@
 
         @pl.when(half == 1)
         def _():
-            lax.fori_loop(1, n_rows, send, 0)
+            lax.fori_loop(1, n_rows, send, 0, unroll=7)
 
     def gram_end(index, count):
         others = gram_recv.at[index, pl.ds(0, n_rows - 1)]
@@ -422,8 +422,8 @@
         return carry
 
     lax.fori_loop(0, nb, take_start, 0, unroll=8)
+    start_halo = send_start_halo()
     gram_begin(0, grams([(0, 0)]))
-    start_halo = send_start_halo()
     for b in range(nb):
         inv_root[b : b + 1, :] = row_sums[table[ROW_END, b], 0:1, :] + col_sums[table[COL_END, b], 0:1, :]
     for copy in deg_copies:

time: 38.8 us -> 38.7 us (level)
  no operation moved by 1% of the time
where the time goes in v4:
time: 38.7 us; the launch traced here: 38.6 us
  Pallas kernels  36 us (93%)
  between operations  1.29 us (3%)
  local copies, waits for them, and re-layouts  1.25 us (3%)
    pallas_call x1, Pallas kernels, local(): pl.pallas_call(functools.partial(kernel, n_rows, n_probe, rows_dev * n_ro...  36 us

profile of v4, /device:TPU:0, one launch (start us, length us, event | category | flops | bytes accessed | tf_op | source)
XLA Modules:
  0.0 38.6 jit_solution(10445967091826285132)
XLA Ops:
  1.3 36.0 %lanczos.1 = (f32[2,32,128]{2,1,0:T(8,128)S(1)}, f32[6,8,128]{2,1,0:T(8,128)S(1)}) custom-call(f32[2,4096]{1,0:T(2,128)} %start_hbm.1, bf16[128,128,128]{2,1,0:T(8,128)(2,1)} %tiles_hbm.1, s32[1,128]{1,0:T(1,128)} %bitcast.8, s32[1,128]{1,0:T(1,128)} %bitcast.9, s32[1]{0:T(128)S(6)} %copy.12.counts_hbm, s32[2,2048]{1,0:T(2,128)} %bound_hbm.1), custom_call_target="tpu_custom_call" | custom-call | tf_op jit(solution)/shard_map/lanczos/pallas_call | solution.py:576
  37.3 0.6 %copy.11 = f32[1,2,32,128]{3,1,2,0:T(2,128)} copy(f32[1,2,32,128]{3,2,1,0:T(8,128)S(1)} %bitcast.6) | data formatting | bytes 65536
  38.0 0.6 %fusion = (f32[3,8,8]{2,1,0:T(8,128)}, f32[3,8,8]{2,1,0:T(8,128)}) fusion(f32[6,8,128]{2,1,0:T(8,128)S(1)} %get-tuple-element.6), kind=kLoop, calls=%fused_computation.1 | loop fusion | bytes 3072 | tf_op jit(solution)/shard_map/slice | solution.py:647
